TPU v7x, 32 devices: a whole 2x2x4 slice. The times are simulated.
32 devices in a mesh: lat: 16 (over z, y, x), head: 2 (over core).
Axes of the slice: x: 2, y: 2, z: 4, core: 2. Of those that a mesh axis runs over, the one named last changes fastest.
Arguments:
- grid_latent: bfloat16 [131072, 512], P('lat'), may hold values from -6 to 6
- mesh_latent: bfloat16 [10240, 512], P('lat'), may hold values from -6 to 6
- neighbours: int32 [10240, 16], P('lat'), may hold values from -1 to 131071, as said below
- edge_bias: bfloat16 [10240, 64], P('lat', 'head'), may hold values from -8 to 384
- query_weight: bfloat16 [512, 512], P(None, 'head'), may hold values from -0.25 to 0.25
- key_weight: bfloat16 [512, 512], P(None, 'head'), may hold values from -0.25 to 0.25
- value_weight: bfloat16 [512, 512], P(None, 'head'), may hold values from -0.25 to 0.25
- out_weight: bfloat16 [512, 512], P('head'), may hold values from -0.25 to 0.25
- norm_gain: bfloat16 [512], P('head'), may hold values from 0.5 to 1.5
Outputs:
- mesh_out: bfloat16 [10240, 512], P('lat', 'head')
Inputs may be any that keep to these rules, and one draw needn't show every extreme that they name: `neighbours`: every neighbour of mesh node m is -1 or lies in [b * 8192 - 2048, (b + 1) * 8192 + 2048) with b = m // 640; both ends of that range (cut to the grid) are named in every draw; slots 0 and 1 are never -1.
All inputs are finite; a program needn't handle non-finite values.
Results may differ from a plain program's by a relative error of at most 0.0075.
Values may be sent and summed in bfloat16 or wider, within the bound.
No kernel may reach another device: no remote copies, remote signals or barrier semaphores. Data moves between devices by JAX's collectives and lax.ppermute only.
A program may use at most 128 MiB of HBM per device.

v0:
```python
import jax
import jax.numpy as jnp
from jax import lax
from jax.sharding import PartitionSpec as P

D = 512
K = 16
HEAD_DIM = 128
HALO = 2048


EPSILON = 1e-05


def extended(block, sides, width):
    for axis, dim in sides:
        count = lax.axis_size(axis)
        forward = [(i, i + 1) for i in range(count - 1)]
        backward = [(target, source) for source, target in forward]
        low = lax.ppermute(
            lax.slice_in_dim(block, block.shape[dim] - width, None, axis=dim), axis, forward
        )
        high = lax.ppermute(lax.slice_in_dim(block, 0, width, axis=dim), axis, backward)
        block = jnp.concatenate([low, block, high], axis=dim)
    return block


def partial_softmax(queries, bias_rows, valid, local, keys, values, local_heads):
    count = queries.shape[0]
    safe_rows = jnp.where(valid, local, 0).reshape(-1)
    key_rows = (
        jnp.take(keys, safe_rows, axis=0)
        .reshape(count, K, local_heads, HEAD_DIM)
        .astype(jnp.float32)
    )
    value_rows = (
        jnp.take(values, safe_rows, axis=0)
        .reshape(count, K, local_heads, HEAD_DIM)
        .astype(jnp.float32)
    )
    query_heads = queries.astype(jnp.float32).reshape(count, local_heads, HEAD_DIM)
    scores = jnp.einsum("nhc,nkhc->nhk", query_heads, key_rows) * HEAD_DIM ** (-0.5)
    scores = scores + bias_rows.astype(jnp.float32).reshape(count, local_heads, K)
    live = valid[:, None, :]
    scores = jnp.where(live, scores, -1e30)
    top_score = jnp.max(scores, axis=2)
    weights = jnp.where(live, jnp.exp(scores - top_score[:, :, None]), 0.0)
    total = jnp.sum(weights, axis=2)
    summed = jnp.einsum("nhk,nkhc->nhc", weights, value_rows)
    return (top_score, total, summed)


def shards(
    grid_latent,
    mesh_latent,
    neighbours,
    edge_bias,
    query_weight,
    key_weight,
    value_weight,
    out_weight,
    norm_gain,
):
    band = grid_latent.shape[0]
    count = mesh_latent.shape[0]
    local_width = key_weight.shape[1]
    local_heads = local_width // HEAD_DIM
    lat_pos = lax.axis_index("lat")
    keys = jnp.dot(grid_latent, key_weight, preferred_element_type=jnp.float32).astype(jnp.bfloat16)
    values = jnp.dot(grid_latent, value_weight, preferred_element_type=jnp.float32).astype(
        jnp.bfloat16
    )
    queries = jnp.dot(mesh_latent, query_weight, preferred_element_type=jnp.float32).astype(
        jnp.bfloat16
    )
    wide_keys, wide_values = (
        extended(keys, (("lat", 0),), HALO),
        extended(values, (("lat", 0),), HALO),
    )
    offset = lat_pos * band - HALO
    valid = neighbours >= 0
    local = jnp.where(valid, neighbours - offset, -1)
    top_score, total, summed = partial_softmax(
        queries, edge_bias, valid, local, wide_keys, wide_values, local_heads
    )
    mixed = summed / total[:, :, None]
    attended = mixed.reshape(count, local_width).astype(jnp.bfloat16)
    projected = jnp.dot(attended, out_weight, preferred_element_type=jnp.float32)
    start = lax.axis_index("head") * local_width
    own_part = lax.psum_scatter(
        projected.astype(jnp.bfloat16), "head", scatter_dimension=1, tiled=True
    ).astype(jnp.float32)
    updated = (
        lax.dynamic_slice_in_dim(mesh_latent, start, local_width, 1).astype(jnp.float32) + own_part
    )
    row_sums, row_squares = lax.psum(
        (jnp.sum(updated, axis=1), jnp.sum(updated * updated, axis=1)), "head"
    )
    mean = row_sums / D
    variance = row_squares / D - mean * mean
    normed = (
        (updated - mean[:, None])
        * lax.rsqrt(variance[:, None] + EPSILON)
        * norm_gain.astype(jnp.float32)
    )
    return normed.astype(jnp.bfloat16)


def solution(mesh):
    in_specs = (
        P("lat", None),
        P("lat", None),
        P("lat", None),
        P("lat", "head"),
        P(None, "head"),
        P(None, "head"),
        P(None, "head"),
        P("head", None),
        P("head"),
    )
    out_specs = P("lat", "head")
    return jax.shard_map(shards, mesh=mesh, in_specs=in_specs, out_specs=out_specs, check_vma=False)
```

profile of v0, /device:TPU:0, one launch (start us, length us, event | category | flops | bytes accessed | tf_op | source)
XLA Modules:
  0.0 268.2 jit_solution(4925674630792918216)
XLA Ops:
  6.5 0.0 copy-start
  6.5 0.0 copy-start.9
  6.5 0.0 reduce-scatter.2.cloned.1.call-start
  6.5 0.9 copy-done
  7.5 0.0 copy-start.8
  7.5 5.9 %convolution_convert_fusion.1 = bf16[8192,256]{1,0:T(8,128)(2,1)S(1)} fusion(bf16[8192,512]{1,0:T(8,128)(2,1)} %param.11, bf16[512,256]{1,0:T(8,128)(2,1)S(1)} %copy-done), kind=kOutput, calls=%fused_computation.5 | convolution fusion | flops 2149580800 | bytes 12845056 | tf_op jit(solution)/shard_map/dot_general | solution.py:69
  13.4 0.0 copy-start.3
  13.4 1.6 fusion.19
  15.0 5.9 %collective-permute-start = (bf16[2048,256]{1,0:T(8,128)(2,1)}, bf16[2048,256]{1,0:T(8,128)(2,1)}, u32[]{:S(2)}, u32[]{:S(2)}) collective-permute-start(bf16[2048,256]{1,0:T(8,128)(2,1)} %get-tuple-element.12), channel_id=1, source_target_pairs={{0,2},{2,4},{4,6},{6,8},{8,10},{10,12},{12,14},{14,16},{16,18},{18... | collective-permute-start | bytes 3145736 | tf_op jit(solution)/shard_map/ppermute | solution.py:20
  20.8 0.0 copy-done.3
  20.8 0.0 copy-start.7
  20.8 0.0 copy-start.4
  20.8 0.0 copy-start.5
  20.8 1.4 collective-permute-start.1
  22.3 0.0 copy-done.9
  22.3 0.0 copy-done.8
  22.3 2.3 convolution_convert_fusion
  24.6 0.0 copy-start.2
  24.6 2.0 copy-done.2
  26.7 1.5 fusion.18
  28.1 4.6 %collective-permute-start.2 = (bf16[2048,256]{1,0:T(8,128)(2,1)}, bf16[2048,256]{1,0:T(8,128)(2,1)S(1)}, u32[]{:S(2)}, u32[]{:S(2)}) collective-permute-start(bf16[2048,256]{1,0:T(8,128)(2,1)} %get-tuple-element.10), channel_id=1, source_target_pairs={{0,2},{2,4},{4,6},{6,8},{8,10},{10,12},{12,14},{14,16},{16,18},{18... | collective-permute-start | bytes 3145736 | tf_op jit(solution)/shard_map/ppermute | solution.py:20
  32.7 1.3 collective-permute-start.3
  34.0 0.0 copy-done.7
  34.1 0.2 copy.11
  34.2 0.1 reshape.34
  34.4 0.0 copy-done.4
  34.4 0.0 copy-done.5
  34.4 0.4 convolution_convert_fusion.3
  34.8 0.9 copy.23
  35.8 52.8 %collective-permute-done = bf16[2048,256]{1,0:T(8,128)(2,1)} collective-permute-done((bf16[2048,256]{1,0:T(8,128)(2,1)}, bf16[2048,256]{1,0:T(8,128)(2,1)}, u32[]{:S(2)}, u32[]{:S(2)}) %collective-permute-start) | collective-permute-done | bytes 1048608 | tf_op jit(solution)/shard_map/ppermute | solution.py:20
  88.6 0.0 collective-permute-done.1
  88.6 8.6 %pad_maximum_fusion = bf16[12288,256]{1,0:T(8,128)(2,1)} fusion(bf16[2048,256]{1,0:T(8,128)(2,1)} %collective-permute-done.1, bf16[8192,256]{1,0:T(8,128)(2,1)} %copy-done.3, bf16[2048,256]{1,0:T(8,128)(2,1)} %collective-permute-done), kind=kLoop, calls=%fused_computation.6 | loop fusion | flops 18874368 | bytes 12582912 | tf_op jit(solution)/shard_map/concatenate | solution.py:24
  97.2 42.0 %gather_fusion = bf16[10240,256]{1,0:T(8,128)(2,1)} fusion(bf16[12288,256]{1,0:T(8,128)(2,1)} %pad_maximum_fusion, s32[10240]{0:T(1024)S(1)} %fusion.15), kind=kCustom, calls=%fused_computation.clone | custom fusion | bytes 10526720 | tf_op jit(solution)/shard_map/jit(_take)/gather | solution.py:32
  139.2 0.0 collective-permute-done.2
  139.2 0.0 collective-permute-done.3
  139.2 12.0 %pad_maximum_fusion.1 = bf16[12288,256]{1,0:T(8,128)(2,1)} fusion(bf16[2048,256]{1,0:T(8,128)(2,1)} %collective-permute-done.3, bf16[8192,256]{1,0:T(8,128)(2,1)} %copy-done.2, bf16[2048,256]{1,0:T(8,128)(2,1)S(1)} %collective-permute-done.2), kind=kLoop, calls=%fused_computation.7 | loop fusion | flops 18874368 | bytes 12582912 | tf_op jit(solution)/shard_map/concatenate | solution.py:24
  151.2 42.0 %gather_fusion.1 = bf16[10240,256]{1,0:T(8,128)(2,1)} fusion(bf16[12288,256]{1,0:T(8,128)(2,1)} %pad_maximum_fusion.1, s32[10240]{0:T(1024)S(1)} %fusion.15), kind=kCustom, calls=%fused_computation.1.clone | custom fusion | bytes 10526720 | tf_op jit(solution)/shard_map/jit(_take)/gather | solution.py:37
  193.2 10.6 %broadcast_select_fusion = (bf16[10240,256]{1,0:T(8,128)(2,1)}, bf16[10240,256]{1,0:T(8,128)(2,1)}) fusion(bf16[10240,256]{1,0:T(8,128)(2,1)} %gather_fusion.1, pred[10240]{0:T(1024)(128)(4,1)S(1)} %compare_and_fusion, bf16[10240,256]{1,0:T(8,128)(2,1)} %gather_fusion), kind=kLoop, calls=%fused_computation.10 | loop fusion | flops 5242880 | bytes 20981760 | tf_op jit(solution)/shard_map/jit(_take)/select_n | solution.py:37
  203.7 8.3 %reshape.35 = bf16[640,16,2,128]{3,2,1,0:T(2,128)(2,1)} reshape(bf16[10240,256]{1,0:T(8,128)(2,1)} %get-tuple-element.15) | data formatting | bytes 10485760 | tf_op jit(solution)/shard_map/reshape | solution.py:33
  212.0 0.0 copy-start.10
  212.0 15.3 %multiply_reduce_fusion = f32[640,2,16]{1,2,0:T(8,128)} fusion(f32[640,2,128]{2,1,0:T(2,128)S(1)} %copy.23, bf16[640,16,2,128]{3,2,1,0:T(2,128)(2,1)} %reshape.35), kind=kLoop, calls=%fused_computation.3 | loop fusion | flops 7843840 | bytes 5980160
  227.3 3.3 %copy.19 = f32[640,2,16]{0,2,1:T(8,128)S(1)} copy(f32[640,2,16]{1,2,0:T(8,128)} %multiply_reduce_fusion) | data formatting | bytes 163840 | tf_op jit(solution)/shard_map/nhc,nkhc->nhk/dot_general | solution.py:42
  230.6 0.0 copy-done.10
  230.6 0.1 fusion.20
  230.7 0.9 copy.20
  231.5 8.5 %reshape.38 = bf16[640,16,2,128]{3,2,1,0:T(2,128)(2,1)} reshape(bf16[10240,256]{1,0:T(8,128)(2,1)} %get-tuple-element.14) | data formatting | bytes 10485760 | tf_op jit(solution)/shard_map/reshape | solution.py:38
  240.1 0.0 copy-start.6
  240.1 0.0 copy-start.11
  240.1 0.0 copy-start.1
  240.1 0.2 copy.12
  240.3 4.0 %fusion.1 = f32[640,2,1,128]{3,2,1,0:T(1,128)S(1)} fusion(bf16[640,2,16,1]{2,3,1,0:T(2,128)(2,1)S(1)} %copy.20, bf16[640,16,2,128]{3,2,1,0:T(2,128)(2,1)} %reshape.38), kind=kOutput, calls=%fused_computation.8 | convolution fusion | flops 5242880 | bytes 5939200 | tf_op jit(solution)/shard_map/nhk,nkhc->nhc/dot_general | solution.py:49
  244.3 0.9 divide_convert_fusion
  245.1 0.0 copy-done.6
  245.1 1.2 convolution_convert_fusion.2
  246.3 0.0 reduce-scatter.2.cloned.1.call-update
  246.3 0.0 copy-done.11
  246.4 9.3 %reduce-scatter.2.cloned.1.call-done = bf16[640,256]{1,0:T(8,128)(2,1)} async-done(((bf16[640,512]{1,0:T(8,128)(2,1)}), bf16[640,256]{1,0:T(8,128)(2,1)}) %reduce-scatter.2.cloned.1.call-update) | async-done | bytes 327696 | tf_op jit(solution)/shard_map/reduce_scatter | solution.py:90
  255.6 1.2 fusion.6
  256.9 2.5 all-reduce
  259.4 1.9 multiply_convert_fusion
  261.3 0.0 copy-done.1
  (6 shorter events, 0.1 us)
Async XLA Ops:
  6.5 1.0 copy-start
  6.5 15.7 %copy-start.9 = (bf16[512,256]{1,0:T(8,128)(2,1)S(1)}, bf16[512,256]{1,0:T(8,128)(2,1)}, u32[]{:S(2)}) copy-start(bf16[512,256]{1,0:T(8,128)(2,1)} %param.17) | copy-start | bytes 786436
  6.5 249.1 %reduce-scatter.2.cloned.1.call-start = ((), (), s32[]{:S(2)}) async-start(), calls=%async_computation.1 | async-start | bytes 983040 | tf_op jit(solution)/shard_map/reduce_scatter | solution.py:90
  7.5 14.8 %copy-start.8 = (bf16[8192,512]{1,0:T(8,128)(2,1)S(1)}, bf16[8192,512]{1,0:T(8,128)(2,1)}, u32[]{:S(2)}) copy-start(bf16[8192,512]{1,0:T(8,128)(2,1)} %param.11) | copy-start | bytes 25165828
  13.4 7.4 %copy-start.3 = (bf16[8192,256]{1,0:T(8,128)(2,1)}, bf16[8192,256]{1,0:T(8,128)(2,1)S(1)}, u32[]{:S(2)}) copy-start(bf16[8192,256]{1,0:T(8,128)(2,1)S(1)} %convolution_convert_fusion.1) | copy-start | bytes 12582916
  15.0 73.7 %collective-permute-start = (bf16[2048,256]{1,0:T(8,128)(2,1)}, bf16[2048,256]{1,0:T(8,128)(2,1)}, u32[]{:S(2)}, u32[]{:S(2)}) collective-permute-start(bf16[2048,256]{1,0:T(8,128)(2,1)} %get-tuple-element.12), channel_id=1, source_target_pairs={{0,2},{2,4},{4,6},{6,8},{8,10},{10,12},{12,14},{14,16},{16,18},{18... | collective-permute-start | bytes 3145736 | tf_op jit(solution)/shard_map/ppermute | solution.py:20
  20.8 13.2 %copy-start.7 = (s32[640,16]{0,1:T(8,128)S(1)}, s32[640,16]{0,1:T(8,128)}, u32[]{:S(2)}) copy-start(s32[640,16]{0,1:T(8,128)} %param.13) | copy-start | bytes 122884
  20.8 13.6 %copy-start.4 = (bf16[640,512]{1,0:T(8,128)(2,1)S(1)}, bf16[640,512]{1,0:T(8,128)(2,1)}, u32[]{:S(2)}) copy-start(bf16[640,512]{1,0:T(8,128)(2,1)} %param.12) | copy-start | bytes 1966084
  20.8 13.6 %copy-start.5 = (bf16[512,256]{1,0:T(8,128)(2,1)S(1)}, bf16[512,256]{1,0:T(8,128)(2,1)}, u32[]{:S(2)}) copy-start(bf16[512,256]{1,0:T(8,128)(2,1)} %param.15) | copy-start | bytes 786436
  20.8 67.8 %collective-permute-start.1 = (bf16[2048,256]{1,0:T(8,128)(2,1)}, bf16[2048,256]{1,0:T(8,128)(2,1)}, u32[]{:S(2)}, u32[]{:S(2)}) collective-permute-start(bf16[2048,256]{1,0:T(8,128)(2,1)} %get-tuple-element.13), channel_id=1, source_target_pairs={{2,0},{4,2},{6,4},{8,6},{10,8},{12,10},{14,12},{16,14},{18,16},{20... | collective-permute-start | bytes 3145736 | tf_op jit(solution)/shard_map/ppermute | solution.py:23
  24.6 2.0 copy-start.2
  28.1 111.1 %collective-permute-start.2 = (bf16[2048,256]{1,0:T(8,128)(2,1)}, bf16[2048,256]{1,0:T(8,128)(2,1)S(1)}, u32[]{:S(2)}, u32[]{:S(2)}) collective-permute-start(bf16[2048,256]{1,0:T(8,128)(2,1)} %get-tuple-element.10), channel_id=1, source_target_pairs={{0,2},{2,4},{4,6},{6,8},{8,10},{10,12},{12,14},{14,16},{16,18},{18... | collective-permute-start | bytes 3145736 | tf_op jit(solution)/shard_map/ppermute | solution.py:20
  32.7 106.5 %collective-permute-start.3 = (bf16[2048,256]{1,0:T(8,128)(2,1)}, bf16[2048,256]{1,0:T(8,128)(2,1)}, u32[]{:S(2)}, u32[]{:S(2)}) collective-permute-start(bf16[2048,256]{1,0:T(8,128)(2,1)} %get-tuple-element.11), channel_id=1, source_target_pairs={{2,0},{4,2},{6,4},{8,6},{10,8},{12,10},{14,12},{16,14},{18,16},{20... | collective-permute-start | bytes 3145736 | tf_op jit(solution)/shard_map/ppermute | solution.py:23
  212.0 18.6 %copy-start.10 = (bf16[640,32]{0,1:T(8,128)(2,1)S(1)}, bf16[640,32]{0,1:T(8,128)(2,1)}, u32[]{:S(2)}) copy-start(bf16[640,32]{0,1:T(8,128)(2,1)} %param.14) | copy-start | bytes 122884
  240.1 5.0 %copy-start.6 = (bf16[256,512]{1,0:T(8,128)(2,1)S(1)}, bf16[256,512]{1,0:T(8,128)(2,1)}, u32[]{:S(2)}) copy-start(bf16[256,512]{1,0:T(8,128)(2,1)} %param.18) | copy-start | bytes 786436
  240.1 6.3 %copy-start.11 = (bf16[256]{0:T(256)(128)(2,1)S(1)}, bf16[256]{0:T(256)(128)(2,1)}, u32[]{:S(2)}) copy-start(bf16[256]{0:T(256)(128)(2,1)} %param.19) | copy-start | bytes 1540
  240.1 21.2 %copy-start.1 = (bf16[512,256]{1,0:T(8,128)(2,1)S(1)}, bf16[512,256]{1,0:T(8,128)(2,1)}, u32[]{:S(2)}) copy-start(bf16[512,256]{1,0:T(8,128)(2,1)} %param.16) | copy-start | bytes 786436
Sparse Core Ops, SparseCore 0:
  246.5 9.1 reduce-scatter.1
where the time goes:
time: 269 us; the launch traced here: 268 us
  local copies, waits for them, and re-layouts  112 us (42%)
  waiting for transfers between devices  62.1 us (23%)
  other arithmetic  50.6 us (19%)
  matrix products  13.8 us (5%)
  between operations  13.6 us (5%)
  starting transfers between devices  13.2 us (5%)
    ppermute x2, waiting for transfers between devices, extended(): lax.ppermute(lax.slice_in_dim(block, block.shape[dim] - width, None, axis...  52.8 us
    gather x1, local copies, waits for them, and re-layouts, partial_softmax(): jnp.take(keys, safe_rows, axis=0).reshape(count, K, local_heads, HEAD_DIM)  42 us
    gather x1, local copies, waits for them, and re-layouts, partial_softmax(): jnp.take(values, safe_rows, axis=0).reshape(count, K, local_heads, HEAD_DIM)  42 us
    concatenate x2, other arithmetic, extended(): block = jnp.concatenate([low, block, high], axis=dim)  20.6 us
    unnamed x1, other arithmetic  15.3 us
    select_n x1, other arithmetic, partial_softmax(): jnp.take(values, safe_rows, axis=0).reshape(count, K, local_heads, HEAD_DIM)  10.6 us
    ppermute x2, starting transfers between devices, extended(): lax.ppermute(lax.slice_in_dim(block, block.shape[dim] - width, None, axis...  10.5 us
    reduce_scatter x1, waiting for transfers between devices, shards(): lax.psum_scatter(projected.astype(jnp.bfloat16), 'head', scatter_dimensio...  9.29 us
  transfers between devices with their start and end apart: 5, of which 2 were waited for; matrix products, arithmetic and copies ran while one was open for 21% of the time, Pallas kernels for 0%

commit v1 on v0

v1 whole, which is shorter than its diff:
```python
import jax
import jax.numpy as jnp
from jax import lax
from jax.experimental import pallas as pl
from jax.experimental.pallas import tpu as pltpu
from jax.sharding import PartitionSpec as P

K = 16
HEAD_DIM = 128
HALO = 2048
LANES = 128
NODES = 64
STAGE = 1024

EPSILON = 1e-05


def attend_kernel(
    rows_ref, head_ref,
    band_ref, low_ref, low_peer_ref, high_ref, high_peer_ref,
    mesh_ref, bias_ref, gain_ref, weights_ref, peer_weights_ref,
    out_ref,
    source_ref, stage_ref, picked_ref, queries_ref, kv_ref, score_ref, mixed_ref, sems,
):
    width = mesh_ref.shape[1]
    half = width // 2
    chunks = width // LANES
    nodes = mesh_ref.shape[0]
    slots = NODES * K
    head = head_ref[0]
    band = band_ref.shape[0]

    pieces = [(band_ref, p * STAGE, HALO + p * STAGE) for p in range(band // STAGE)]
    for mine, peer, base in ((low_ref, low_peer_ref, 0), (high_ref, high_peer_ref, HALO + band)):
        part = mine.shape[0]
        for p in range(part // STAGE):
            pieces.append((mine, p * STAGE, base + head * part + p * STAGE))
            pieces.append((peer, p * STAGE, base + (1 - head) * part + p * STAGE))

    def copy(n):
        ref, start, _ = pieces[n]
        return pltpu.make_async_copy(
            ref.at[pl.ds(start, STAGE), :], stage_ref.at[n % 2], sems.at[n % 2]
        )

    copy(0).start()
    for n in range(len(pieces)):
        if n + 1 < len(pieces):
            copy(n + 1).start()
        copy(n).wait()
        target = pieces[n][2]

        def convert(step, _, n=n, target=target):
            rows = 64
            block = stage_ref[n % 2, pl.ds(pl.multiple_of(step * rows, rows), rows), :]
            block = block.astype(jnp.float32)
            start = pl.multiple_of((target + step * rows) * chunks, rows * chunks)
            for c in range(chunks):
                source_ref[pl.ds(start + c, rows, stride=chunks), :] = block[
                    :, c * LANES : (c + 1) * LANES
                ]
            return 0

        lax.fori_loop(0, STAGE // 64, convert, 0)

    def weight(ref, n):
        return ref[pl.ds(n * width, width), :]

    for part, ref in enumerate((weights_ref, peer_weights_ref)):
        q = jnp.dot(mesh_ref[...], weight(ref, 0), preferred_element_type=jnp.float32)
        queries_ref[:, part * half : (part + 1) * half] = q.astype(jnp.bfloat16).astype(
            jnp.float32
        ) * HEAD_DIM ** (-0.5)

    lane = lax.broadcasted_iota(jnp.int32, (half, half), 0) // HEAD_DIM
    same = (lane == lax.broadcasted_iota(jnp.int32, (half, half), 1) // HEAD_DIM)
    ones = jnp.where(same, 1.0, 0.0).astype(jnp.bfloat16)

    def block_step(b, _):
        def pick(step, _):
            unroll = 32
            base = b * slots + step * unroll
            to = pl.multiple_of(step * unroll * chunks, unroll * chunks)
            for u in range(unroll):
                row = pl.multiple_of(rows_ref[base + u], chunks)
                picked_ref[pl.ds(to + u * chunks, chunks), :] = source_ref[pl.ds(row, chunks), :]
            return 0

        lax.fori_loop(0, slots // 32, pick, 0)
        latents = jnp.concatenate(
            [
                picked_ref[pl.ds(c, slots, stride=chunks), :].astype(jnp.bfloat16)
                for c in range(chunks)
            ],
            axis=1,
        )
        for part, ref in enumerate((weights_ref, peer_weights_ref)):
            for n in range(2):
                r = jnp.dot(latents, weight(ref, 1 + n), preferred_element_type=jnp.float32)
                kv_ref[n, :, part * half : (part + 1) * half] = r.astype(jnp.bfloat16)
        first = pl.multiple_of(b * NODES, NODES)
        q = queries_ref[pl.ds(first, NODES), :]
        for k in range(K):
            product = kv_ref[0, k * NODES : (k + 1) * NODES, :].astype(jnp.float32) * q
            score_ref[k * NODES : (k + 1) * NODES, :] = product
        for part in range(2):
            product = score_ref[:, part * half : (part + 1) * half]
            upper = product.astype(jnp.bfloat16)
            lower = (product - upper.astype(jnp.float32)).astype(jnp.bfloat16)
            score_ref[:, part * half : (part + 1) * half] = jnp.dot(
                upper, ones, preferred_element_type=jnp.float32
            ) + jnp.dot(lower, ones, preferred_element_type=jnp.float32)

        def mix(step, _):
            tile = 16
            at = pl.multiple_of(step * tile, tile)
            for h in range(chunks):
                cols = slice(h * LANES, (h + 1) * LANES)
                scores = []
                for k in range(K):
                    c = h * K + k
                    bias = bias_ref[pl.ds(first + at, tile), c : c + 1]
                    scores.append(
                        score_ref[pl.ds(k * NODES + at, tile), cols]
                        + jnp.broadcast_to(bias, (tile, LANES))
                    )
                top = scores[0]
                for k in range(1, K):
                    top = jnp.maximum(top, scores[k])
                total = jnp.zeros((tile, LANES), jnp.float32)
                summed = jnp.zeros((tile, LANES), jnp.float32)
                for k in range(K):
                    w = jnp.exp(scores[k] - top)
                    total = total + w
                    summed = summed + w * kv_ref[1, pl.ds(k * NODES + at, tile), cols].astype(
                        jnp.float32
                    )
                mixed_ref[pl.ds(first + at, tile), cols] = (summed / total).astype(jnp.bfloat16)
            return 0

        lax.fori_loop(0, NODES // 16, mix, 0)
        return 0

    lax.fori_loop(0, nodes // NODES, block_step, 0)

    for part in range(2):
        cols = slice(part * half, (part + 1) * half)
        projected = jnp.dot(
            mixed_ref[:, :half],
            weights_ref[pl.ds((3 * width + part * half), half), :],
            preferred_element_type=jnp.float32,
        ) + jnp.dot(
            mixed_ref[:, half:],
            peer_weights_ref[pl.ds((3 * width + part * half), half), :],
            preferred_element_type=jnp.float32,
        )
        queries_ref[:, cols] = mesh_ref[:, cols].astype(jnp.float32) + projected
    updated = queries_ref[...]
    mean = jnp.sum(updated, axis=1, keepdims=True) / width
    variance = jnp.sum(updated * updated, axis=1, keepdims=True) / width - mean * mean
    normed = (updated - mean) * lax.rsqrt(variance + EPSILON) * gain_ref[...]
    out_ref[0] = normed[:, :half].astype(jnp.bfloat16)
    out_ref[1] = normed[:, half:].astype(jnp.bfloat16)


def shards(
    grid_latent,
    mesh_latent,
    neighbours,
    edge_bias,
    query_weight,
    key_weight,
    value_weight,
    out_weight,
    norm_gain,
):
    band, width = grid_latent.shape
    count = mesh_latent.shape[0]
    nodes = count // 2
    half = width // 2
    part = HALO // 2
    head = lax.axis_index("head")
    lat_pos = lax.axis_index("lat")
    lats = lax.axis_size("lat")
    forward = [(i, i + 1) for i in range(lats - 1)]
    backward = [(i + 1, i) for i in range(lats - 1)]
    swap = [(0, 1), (1, 0)]

    low = lax.ppermute(
        lax.dynamic_slice_in_dim(grid_latent, band - HALO + head * part, part, 0), "lat", forward
    )
    high = lax.ppermute(
        lax.dynamic_slice_in_dim(grid_latent, head * part, part, 0), "lat", backward
    )

    packed = jnp.concatenate(
        [query_weight, key_weight, value_weight, out_weight[:, :half], out_weight[:, half:]], axis=0
    )
    peer_packed = lax.ppermute(packed, "head", swap)
    theirs = lax.dynamic_slice_in_dim(edge_bias, (1 - head) * nodes, nodes, 0)
    mine = lax.dynamic_slice_in_dim(edge_bias, head * nodes, nodes, 0)
    peer_bias = lax.ppermute(theirs, "head", swap)
    peer_gain = lax.ppermute(norm_gain, "head", swap)
    gain = jnp.where(
        head == 0,
        jnp.concatenate([norm_gain, peer_gain]),
        jnp.concatenate([peer_gain, norm_gain]),
    ).astype(jnp.float32)[None, :]

    my_mesh = lax.dynamic_slice_in_dim(mesh_latent, head * nodes, nodes, 0)
    my_neighbours = lax.dynamic_slice_in_dim(neighbours, head * nodes, nodes, 0)
    valid = my_neighbours >= 0
    bias = jnp.where(
        jnp.tile(valid, (1, width // HEAD_DIM)),
        jnp.concatenate([mine, peer_bias], axis=1).astype(jnp.float32),
        -1e30,
    )
    rows = jnp.where(valid, my_neighbours - (lat_pos * band - HALO), HALO) * (width // LANES)
    rows = rows.reshape(nodes // NODES, NODES, K).transpose(0, 2, 1).reshape(-1)

    low_peer = lax.ppermute(low, "head", swap)
    high_peer = lax.ppermute(high, "head", swap)

    smem = pl.BlockSpec(memory_space=pltpu.SMEM)
    anywhere = pl.BlockSpec(memory_space=pl.ANY)
    vmem = pl.BlockSpec(memory_space=pltpu.VMEM)
    slots = NODES * K
    halves = pl.pallas_call(
        attend_kernel,
        out_shape=jax.ShapeDtypeStruct((2, nodes, half), jnp.bfloat16),
        in_specs=[smem, smem] + [anywhere] * 5 + [vmem] * 5,
        out_specs=vmem,
        scratch_shapes=[
            pltpu.VMEM(((band + 2 * HALO) * (width // LANES), LANES), jnp.float32),
            pltpu.VMEM((2, STAGE, width), jnp.bfloat16),
            pltpu.VMEM((slots * (width // LANES), LANES), jnp.float32),
            pltpu.VMEM((nodes, width), jnp.float32),
            pltpu.VMEM((2, slots, width), jnp.bfloat16),
            pltpu.VMEM((slots, width), jnp.float32),
            pltpu.VMEM((nodes, width), jnp.bfloat16),
            pltpu.SemaphoreType.DMA((2,)),
        ],
        compiler_params=pltpu.CompilerParams(vmem_limit_bytes=56 * 1024 * 1024),
        name="attend",
    )(
        rows, head.reshape(1).astype(jnp.int32),
        grid_latent, low, low_peer, high, high_peer,
        my_mesh, bias, gain, packed, peer_packed,
    )
    keep = lax.dynamic_index_in_dim(halves, head, 0, keepdims=False)
    give = lax.dynamic_index_in_dim(halves, 1 - head, 0, keepdims=False)
    got = lax.ppermute(give, "head", swap)
    return jnp.where(
        head == 0, jnp.concatenate([keep, got], axis=0), jnp.concatenate([got, keep], axis=0)
    )


def solution(mesh):
    in_specs = (
        P("lat", None),
        P("lat", None),
        P("lat", None),
        P("lat", "head"),
        P(None, "head"),
        P(None, "head"),
        P(None, "head"),
        P("head", None),
        P("head"),
    )
    out_specs = P("lat", "head")
    return jax.shard_map(shards, mesh=mesh, in_specs=in_specs, out_specs=out_specs, check_vma=False)
```

time: 269 us -> 97.3 us (0.36)
  local copies, waits for them, and re-layouts: 112 us -> 11 us
  other arithmetic: 50.6 us -> 3.06 us
  Pallas kernels: 0 us -> 33.2 us
  waiting for transfers between devices: 62.1 us -> 41.7 us
  matrix products: 13.8 us -> 0 us
  between operations: 13.6 us -> 0.11 us
  starting transfers between devices: 13.2 us -> 7.45 us
    gather x2 -> x0, local copies, waits for them, and re-layouts: 83.9 us -> none  [the longest x1 42 us: partial_softmax(): jnp.take(keys, safe_rows, axis=0).reshape(count, K, local_heads, HEAD_DIM)]
    pallas_call x0 -> x1, Pallas kernels: none -> 33.2 us  [shards(): pl.pallas_call(attend_kernel, out_shape=jax.ShapeDtypeStruct((2, nodes, h...]
    concatenate x2 -> x0, other arithmetic: 20.6 us -> none  [extended(): block = jnp.concatenate([low, block, high], axis=dim)]
    reshape x3 -> x2, local copies, waits for them, and re-layouts: 17 us -> 0.75 us  [shards(): rows = rows.reshape(nodes // NODES, NODES, K).transpose(0, 2, 1).reshape(-1)]
    unnamed x1 -> x0, other arithmetic: 15.3 us -> none
    dot_general x5 -> x0, matrix products: 13.8 us -> none  [the longest x1 5.88 us: shards(): jnp.dot(grid_latent, key_weight, preferred_element_type=jnp.float32)]
    ppermute x4 -> x8, waiting for transfers between devices: 52.8 us -> 41.7 us  [the longest x1 38.7 us: shards(): lax.ppermute(lax.dynamic_slice_in_dim(grid_latent, band - HALO + head * p...]
    reduce_scatter x1 -> x0, waiting for transfers between devices: 9.29 us -> none  [shards(): lax.psum_scatter(projected.astype(jnp.bfloat16), 'head', scatter_dimensio...]
  transfers between devices with their start and end apart: 5 -> 8, of which waited for: 2 -> 3; matrix products, arithmetic and copies ran while one was open for 21% -> 11% of each run, Pallas kernels for 0% -> 0%
where the time goes in v1:
time: 97.3 us; the launch traced here: 96.6 us
  waiting for transfers between devices  41.7 us (43%)
  Pallas kernels  33.2 us (34%)
  local copies, waits for them, and re-layouts  11 us (11%)
  starting transfers between devices  7.45 us (8%)
  other arithmetic  3.06 us (3%)
    ppermute x1, waiting for transfers between devices, shards(): lax.ppermute(lax.dynamic_slice_in_dim(grid_latent, band - HALO + head * p...  38.7 us
    pallas_call x1, Pallas kernels, shards(): pl.pallas_call(attend_kernel, out_shape=jax.ShapeDtypeStruct((2, nodes, h...  33.2 us
    ppermute x1, starting transfers between devices, shards(): lax.ppermute(lax.dynamic_slice_in_dim(grid_latent, band - HALO + head * p...  4.94 us
    unnamed x12, local copies, waits for them, and re-layouts  4.09 us
    ppermute x1, waiting for transfers between devices, shards(): lax.ppermute(lax.dynamic_slice_in_dim(grid_latent, head * part, part, 0),...  2.05 us
  transfers between devices with their start and end apart: 8, of which 3 were waited for; matrix products, arithmetic and copies ran while one was open for 11% of the time, Pallas kernels for 0%

profile of v1, /device:TPU:0, one launch (start us, length us, event | category | flops | bytes accessed | tf_op | source)
XLA Modules:
  0.0 96.6 jit_solution(5415042026683712563)
XLA Ops:
  0.0 0.0 copy-start
  0.0 1.7 %constant_dynamic-slice_fusion.3 = (bf16[1024,512]{1,0:T(8,128)(2,1)S(1)}, bf16[1024,512]{1,0:T(8,128)(2,1)S(1)}) fusion(bf16[8192,512]{1,0:T(8,128)(2,1)} %band_ref.1, s32[]{:T(128)S(6)} %select_n.56, s32[]{:T(128)S(6)} %select_n.55), kind=kLoop, calls=%fused_computation.16 | loop fusion | bytes 4194312 | tf_op jit(solution)/shard_map/dynamic_slice | solution.py:193
  1.7 4.9 %collective-permute-start = (bf16[1024,512]{1,0:T(8,128)(2,1)S(1)}, bf16[1024,512]{1,0:T(8,128)(2,1)S(1)}, u32[]{:S(2)}, u32[]{:S(2)}) collective-permute-start(bf16[1024,512]{1,0:T(8,128)(2,1)S(1)} %get-tuple-element.8), channel_id=1, source_target_pairs={{0,2},{2,4},{4,6},{6,8},{8,10},{10,12},{12,14},{14,16},{16,18},{18... | collective-permute-start | bytes 3145736 | tf_op jit(solution)/shard_map/ppermute | solution.py:189
  6.7 1.3 %collective-permute-start.2 = (bf16[1024,512]{1,0:T(8,128)(2,1)S(1)}, bf16[1024,512]{1,0:T(8,128)(2,1)}, u32[]{:S(2)}, u32[]{:S(2)}) collective-permute-start(bf16[1024,512]{1,0:T(8,128)(2,1)S(1)} %get-tuple-element.7), channel_id=1, source_target_pairs={{2,0},{4,2},{6,4},{8,6},{10,8},{12,10},{14,12},{16,14},{18,16},{20... | collective-permute-start | bytes 3145736 | tf_op jit(solution)/shard_map/ppermute | solution.py:192
  8.0 1.0 %constant_dynamic-update-slice_fusion.2 = bf16[2048,256]{1,0:T(8,128)(2,1)S(1)} fusion(bf16[512,256]{1,0:T(8,128)(2,1)} %param.13), kind=kLoop, calls=%fused_computation.10 | loop fusion | bytes 524288
  9.0 1.0 %constant_dynamic-update-slice_fusion.1 = bf16[2048,256]{1,0:T(8,128)(2,1)S(1)} fusion(bf16[2048,256]{1,0:T(8,128)(2,1)S(1)} %constant_dynamic-update-slice_fusion.2, bf16[512,256]{1,0:T(8,128)(2,1)} %param.14), kind=kLoop, calls=%fused_computation.9 | loop fusion | bytes 524288
  9.9 1.0 %constant_dynamic-update-slice_fusion = bf16[2048,256]{1,0:T(8,128)(2,1)S(1)} fusion(bf16[2048,256]{1,0:T(8,128)(2,1)S(1)} %constant_dynamic-update-slice_fusion.1, bf16[512,256]{1,0:T(8,128)(2,1)} %param.15), kind=kLoop, calls=%fused_computation.8 | loop fusion | bytes 524288
  10.9 0.9 slice_dynamic-update-slice_fusion.1
  11.8 0.9 slice_dynamic-update-slice_fusion.weights_ref
  12.8 0.0 copy-start.1
  12.8 0.1 collective-permute-start.6
  12.8 38.7 %collective-permute-done.low_ref = bf16[1024,512]{1,0:T(8,128)(2,1)S(1)} collective-permute-done((bf16[1024,512]{1,0:T(8,128)(2,1)S(1)}, bf16[1024,512]{1,0:T(8,128)(2,1)S(1)}, u32[]{:S(2)}, u32[]{:S(2)}) %collective-permute-start) | collective-permute-done | bytes 1048608 | tf_op jit(solution)/shard_map/ppermute | solution.py:189
  51.5 0.0 copy-start.2
  51.5 0.0 collective-permute-start.1
  51.5 2.0 %collective-permute-done.2.high_ref = bf16[1024,512]{1,0:T(8,128)(2,1)} collective-permute-done((bf16[1024,512]{1,0:T(8,128)(2,1)S(1)}, bf16[1024,512]{1,0:T(8,128)(2,1)}, u32[]{:S(2)}, u32[]{:S(2)}) %collective-permute-start.2) | collective-permute-done | bytes 1048608 | tf_op jit(solution)/shard_map/ppermute | solution.py:192
  53.5 0.0 collective-permute-start.3
  53.6 0.9 constant_dynamic-slice_fusion.1
  54.5 0.1 copy.18
  54.6 0.6 collective-permute-start.4
  55.2 0.1 collective-permute-start.5
  55.2 0.7 concatenate.37
  55.9 0.1 copy.17
  56.0 0.8 select_multiply_fusion
  56.9 0.1 copy.16
  57.0 0.0 copy-done
  57.0 0.8 constant_dynamic-slice_fusion.2.mesh_ref
  57.8 0.1 reshape.71
  57.9 0.7 reshape.72.rows_ref
  58.6 0.0 collective-permute-done.5
  58.6 0.6 fusion.gain_ref
  59.2 0.0 collective-permute-done.4
  59.2 0.8 convert_select_fusion.bias_ref
  59.9 0.0 collective-permute-done.6.peer_weights_ref
  59.9 0.0 collective-permute-done.1.low_peer_ref
  59.9 0.0 collective-permute-done.3.high_peer_ref
  60.0 0.0 copy-done.1
  60.0 0.0 copy-done.2
  60.0 33.2 %attend.1 = bf16[2,320,256]{2,1,0:T(8,128)(2,1)} custom-call(s32[5120]{0:T(1024)} %reshape.72.rows_ref, s32[1]{0:T(128)} %bitcast.1.head_ref, bf16[8192,512]{1,0:T(8,128)(2,1)} %band_ref.1, bf16[1024,512]{1,0:T(8,128)(2,1)} %copy-done.2, bf16[1024,512]{1,0:T(8,128)(2,1)} %collective-permute-done.1.low_peer_ref, ...), custom_call_target="tpu_custom_call" | custom-call | tf_op jit(solution)/shard_map/attend/pallas_call | solution.py:228
  93.2 1.0 %dynamic-slice_bitcast_fusion.1 = (bf16[320,256]{1,0:T(8,128)(2,1)S(1)}, bf16[320,256]{1,0:T(8,128)(2,1)S(1)}) fusion(bf16[2,320,256]{2,1,0:T(8,128)(2,1)} %attend.1, s32[]{:T(128)S(6)} %select_n.61, s32[]{:T(128)S(6)} %select_n.62), kind=kLoop, calls=%fused_computation.2 | loop fusion | bytes 655368 | tf_op jit(solution)/shard_map/jit(dynamic_index_in_dim)/squeeze | solution.py:250
  94.3 0.5 collective-permute-start.7
  94.7 1.0 %collective-permute-done.7 = bf16[320,256]{1,0:T(8,128)(2,1)S(1)} collective-permute-done((bf16[320,256]{1,0:T(8,128)(2,1)S(1)}, bf16[320,256]{1,0:T(8,128)(2,1)S(1)}, u32[]{:S(2)}, u32[]{:S(2)}) %collective-permute-start.7) | collective-permute-done | bytes 163872 | tf_op jit(solution)/shard_map/ppermute | solution.py:252
  95.8 0.8 maximum_select_fusion
  (3 shorter events, 0.0 us)
Async XLA Ops:
  0.0 57.0 %copy-start = (bf16[640,512]{1,0:T(8,128)(2,1)S(1)}, bf16[640,512]{1,0:T(8,128)(2,1)}, u32[]{:S(2)}) copy-start(bf16[640,512]{1,0:T(8,128)(2,1)} %param.10) | copy-start | bytes 1966084
  1.7 49.7 %collective-permute-start = (bf16[1024,512]{1,0:T(8,128)(2,1)S(1)}, bf16[1024,512]{1,0:T(8,128)(2,1)S(1)}, u32[]{:S(2)}, u32[]{:S(2)}) collective-permute-start(bf16[1024,512]{1,0:T(8,128)(2,1)S(1)} %get-tuple-element.8), channel_id=1, source_target_pairs={{0,2},{2,4},{4,6},{6,8},{8,10},{10,12},{12,14},{14,16},{16,18},{18... | collective-permute-start | bytes 3145736 | tf_op jit(solution)/shard_map/ppermute | solution.py:189
  6.7 46.9 %collective-permute-start.2 = (bf16[1024,512]{1,0:T(8,128)(2,1)S(1)}, bf16[1024,512]{1,0:T(8,128)(2,1)}, u32[]{:S(2)}, u32[]{:S(2)}) collective-permute-start(bf16[1024,512]{1,0:T(8,128)(2,1)S(1)} %get-tuple-element.7), channel_id=1, source_target_pairs={{2,0},{4,2},{6,4},{8,6},{10,8},{12,10},{14,12},{16,14},{18,16},{20... | collective-permute-start | bytes 3145736 | tf_op jit(solution)/shard_map/ppermute | solution.py:192
  12.8 47.2 %copy-start.1 = (bf16[2048,256]{1,0:T(8,128)(2,1)}, bf16[2048,256]{1,0:T(8,128)(2,1)S(1)}, u32[]{:S(2)}) copy-start(bf16[2048,256]{1,0:T(8,128)(2,1)S(1)} %slice_dynamic-update-slice_fusion.weights_ref) | copy-start | bytes 3145732
  12.8 47.2 %collective-permute-start.6 = (bf16[2048,256]{1,0:T(8,128)(2,1)S(1)}, bf16[2048,256]{1,0:T(8,128)(2,1)}, u32[]{:S(2)}, u32[]{:S(2)}) collective-permute-start(bf16[2048,256]{1,0:T(8,128)(2,1)S(1)} %slice_dynamic-update-slice_fusion.weights_ref), channel_id=1, source_target_pairs={{0,1},{1,0},{2,3},{3,2},{4,5},{5,4},{6,7},{7,6},{8,9},{9,8},{10,11... | collective-permute-start | bytes 3145736 | tf_op jit(solution)/shard_map/ppermute | solution.py:199
  51.5 8.5 %copy-start.2 = (bf16[1024,512]{1,0:T(8,128)(2,1)}, bf16[1024,512]{1,0:T(8,128)(2,1)S(1)}, u32[]{:S(2)}) copy-start(bf16[1024,512]{1,0:T(8,128)(2,1)S(1)} %collective-permute-done.low_ref) | copy-start | bytes 3145732
  51.5 8.4 %collective-permute-start.1 = (bf16[1024,512]{1,0:T(8,128)(2,1)S(1)}, bf16[1024,512]{1,0:T(8,128)(2,1)}, u32[]{:S(2)}, u32[]{:S(2)}) collective-permute-start(bf16[1024,512]{1,0:T(8,128)(2,1)S(1)} %collective-permute-done.low_ref), channel_id=1, source_target_pairs={{0,1},{1,0},{2,3},{3,2},{4,5},{5,4},{6,7},{7,6},{8,9},{9,8},{10,11... | collective-permute-start | bytes 3145736 | tf_op jit(solution)/shard_map/ppermute | solution.py:221
  53.5 6.4 %collective-permute-start.3 = (bf16[1024,512]{1,0:T(8,128)(2,1)}, bf16[1024,512]{1,0:T(8,128)(2,1)}, u32[]{:S(2)}, u32[]{:S(2)}) collective-permute-start(bf16[1024,512]{1,0:T(8,128)(2,1)} %collective-permute-done.2.high_ref), channel_id=1, source_target_pairs={{0,1},{1,0},{2,3},{3,2},{4,5},{5,4},{6,7},{7,6},{8,9},{9,8},{10,11... | collective-permute-start | bytes 3145736 | tf_op jit(solution)/shard_map/ppermute | solution.py:222
  54.6 4.6 %collective-permute-start.4 = (bf16[320,32]{1,0:T(8,128)(2,1)S(1)}, bf16[320,32]{1,0:T(8,128)(2,1)S(1)}, u32[]{:S(2)}, u32[]{:S(2)}) collective-permute-start(bf16[320,32]{1,0:T(8,128)(2,1)S(1)} %copy.18), channel_id=1, source_target_pairs={{0,1},{1,0},{2,3},{3,2},{4,5},{5,4},{6,7},{7,6},{8,9},{9,8},{10,11... | collective-permute-start | bytes 61448 | tf_op jit(solution)/shard_map/ppermute | solution.py:202
  55.2 3.4 %collective-permute-start.5 = (bf16[256]{0:T(256)(128)(2,1)}, bf16[256]{0:T(256)(128)(2,1)S(1)}, u32[]{:S(2)}, u32[]{:S(2)}) collective-permute-start(bf16[256]{0:T(256)(128)(2,1)} %param.17), channel_id=1, source_target_pairs={{0,1},{1,0},{2,3},{3,2},{4,5},{5,4},{6,7},{7,6},{8,9},{9,8},{10,11... | collective-permute-start | bytes 1544 | tf_op jit(solution)/shard_map/ppermute | solution.py:203
  94.3 1.5 %collective-permute-start.7 = (bf16[320,256]{1,0:T(8,128)(2,1)S(1)}, bf16[320,256]{1,0:T(8,128)(2,1)S(1)}, u32[]{:S(2)}, u32[]{:S(2)}) collective-permute-start(bf16[320,256]{1,0:T(8,128)(2,1)S(1)} %get-tuple-element.10), channel_id=1, source_target_pairs={{0,1},{1,0},{2,3},{3,2},{4,5},{5,4},{6,7},{7,6},{8,9},{9,8},{10,11... | collective-permute-start | bytes 491528 | tf_op jit(solution)/shard_map/ppermute | solution.py:252

commit v2 on v1

v2 whole, which is shorter than its diff:
```python
import jax
import jax.numpy as jnp
from jax import lax
from jax.experimental import pallas as pl
from jax.experimental.pallas import tpu as pltpu
from jax.sharding import PartitionSpec as P


K = 16
HEAD_DIM = 128
HALO = 2048
LANES = 128
NODES = 64
STAGE = 1024
FEW = 4

EPSILON = 1e-05


def stage(pieces, stage_ref, source_ref, sems):
    width = stage_ref.shape[2]
    chunks = width // LANES

    def copy(n):
        ref, start, _ = pieces[n]
        return pltpu.make_async_copy(
            ref.at[pl.ds(start, STAGE), :], stage_ref.at[n % 2], sems.at[n % 2]
        )

    copy(0).start()
    for n in range(len(pieces)):
        if n + 1 < len(pieces):
            copy(n + 1).start()
        copy(n).wait()
        target = pieces[n][2]

        def convert(step, _, n=n, target=target):
            rows = 64
            block = stage_ref[n % 2, pl.ds(pl.multiple_of(step * rows, rows), rows), :]
            block = block.astype(jnp.float32)
            start = pl.multiple_of((target + step * rows) * chunks, rows * chunks)
            for c in range(chunks):
                source_ref[pl.ds(start + c, rows, stride=chunks), :] = block[
                    :, c * LANES : (c + 1) * LANES
                ]
            return 0

        lax.fori_loop(0, STAGE // 64, convert, 0)


def head_sums(half):
    lane = lax.broadcasted_iota(jnp.int32, (half, half), 0) // HEAD_DIM
    same = lane == lax.broadcasted_iota(jnp.int32, (half, half), 1) // HEAD_DIM
    return jnp.where(same, 1.0, 0.0).astype(jnp.bfloat16)


def attend_slots(
    b, begin, taken, fresh, rows_ref, bias_ref, queries_ref, weights, source_ref,
    picked_ref, kv_ref, score_ref, top_ref, total_ref, summed_ref, ones,
):
    width = queries_ref.shape[1]
    half = width // 2
    chunks = width // LANES
    slots = taken * NODES
    unroll = 32

    def pick(step, _):
        base = (b * K + begin) * NODES + step * unroll
        to = pl.multiple_of(step * unroll * chunks, unroll * chunks)
        for u in range(unroll):
            row = pl.multiple_of(rows_ref[base + u], chunks)
            picked_ref[pl.ds(to + u * chunks, chunks), :] = source_ref[pl.ds(row, chunks), :]
        return 0

    lax.fori_loop(0, slots // unroll, pick, 0)
    latents = jnp.concatenate(
        [picked_ref[pl.ds(c, slots, stride=chunks), :].astype(jnp.bfloat16) for c in range(chunks)],
        axis=1,
    )
    for part, ref in enumerate(weights):
        for n in range(2):
            r = jnp.dot(
                latents, ref[pl.ds((1 + n) * width, width), :], preferred_element_type=jnp.float32
            )
            kv_ref[n, :, part * half : (part + 1) * half] = r.astype(jnp.bfloat16)
    first = pl.multiple_of(b * NODES, NODES)
    q = queries_ref[pl.ds(first, NODES), :]
    for k in range(taken):
        near = slice(k * NODES, (k + 1) * NODES)
        score_ref[near, :] = kv_ref[0, near, :].astype(jnp.float32) * q
    for part in range(2):
        cols = slice(part * half, (part + 1) * half)
        product = score_ref[:, cols]
        upper = product.astype(jnp.bfloat16)
        lower = (product - upper.astype(jnp.float32)).astype(jnp.bfloat16)
        score_ref[:, cols] = jnp.dot(upper, ones, preferred_element_type=jnp.float32) + jnp.dot(
            lower, ones, preferred_element_type=jnp.float32
        )

    tile = 16

    def mix(step, _):
        at = pl.multiple_of(step * tile, tile)
        here = pl.ds(first + at, tile)
        for h in range(chunks):
            cols = slice(h * LANES, (h + 1) * LANES)
            scores = []
            for k in range(taken):
                bias = bias_ref[begin // taken, here, h * taken + k : h * taken + k + 1]
                scores.append(
                    score_ref[pl.ds(k * NODES + at, tile), cols]
                    + jnp.broadcast_to(bias, (tile, LANES))
                )
            top = scores[0]
            for score in scores[1:]:
                top = jnp.maximum(top, score)
            if fresh:
                total = jnp.zeros((tile, LANES), jnp.float32)
                summed = jnp.zeros((tile, LANES), jnp.float32)
            else:
                before = top_ref[here, cols]
                top = jnp.maximum(top, before)
                fade = jnp.exp(before - top)
                total = total_ref[here, cols] * fade
                summed = summed_ref[here, cols] * fade
            for k in range(taken):
                w = jnp.exp(scores[k] - top)
                total = total + w
                summed = summed + w * kv_ref[1, pl.ds(k * NODES + at, tile), cols].astype(
                    jnp.float32
                )
            top_ref[here, cols] = top
            total_ref[here, cols] = total
            summed_ref[here, cols] = summed
        return 0

    lax.fori_loop(0, NODES // tile, mix, 0)


def band_kernel(
    rows_ref, band_ref, mesh_ref, bias_ref, weights_ref, peer_weights_ref,
    queries_ref, top_ref, total_ref, summed_ref,
    source_ref, stage_ref, picked_ref, kv_ref, score_ref, sems,
):
    nodes, width = mesh_ref.shape
    half = width // 2
    weights = (weights_ref, peer_weights_ref)
    pieces = [(band_ref, p * STAGE, p * STAGE) for p in range(band_ref.shape[0] // STAGE)]
    stage(pieces, stage_ref, source_ref, sems)
    for part, ref in enumerate(weights):
        q = jnp.dot(mesh_ref[...], ref[pl.ds(0, width), :], preferred_element_type=jnp.float32)
        queries_ref[:, part * half : (part + 1) * half] = q.astype(jnp.bfloat16).astype(
            jnp.float32
        ) * HEAD_DIM ** (-0.5)
    ones = head_sums(half)

    def block_step(b, _):
        attend_slots(
            b, 0, K, True, rows_ref, bias_ref, queries_ref, weights, source_ref,
            picked_ref, kv_ref, score_ref, top_ref, total_ref, summed_ref, ones,
        )
        return 0

    lax.fori_loop(0, nodes // NODES, block_step, 0)


def halo_kernel(
    rows_ref, trips_ref, head_ref, low_ref, low_peer_ref, high_ref, high_peer_ref,
    mesh_ref, bias_ref, gain_ref, weights_ref, peer_weights_ref,
    queries_ref, top_in_ref, total_in_ref, summed_in_ref,
    keep_ref, give_ref,
    source_ref, stage_ref, picked_ref, kv_ref, score_ref, top_ref, total_ref, summed_ref,
    mixed_ref, sems,
):
    nodes, width = mesh_ref.shape
    half = width // 2
    head = head_ref[0]
    weights = (weights_ref, peer_weights_ref)
    pieces = []
    for mine, peer, base in ((low_ref, low_peer_ref, 0), (high_ref, high_peer_ref, HALO)):
        part = mine.shape[0]
        for p in range(part // STAGE):
            pieces.append((mine, p * STAGE, base + head * part + p * STAGE))
            pieces.append((peer, p * STAGE, base + (1 - head) * part + p * STAGE))
    stage(pieces, stage_ref, source_ref, sems)
    top_ref[...] = top_in_ref[...]
    total_ref[...] = total_in_ref[...]
    summed_ref[...] = summed_in_ref[...]
    ones = head_sums(half)

    def block_step(b, _):
        def trip(t, _):
            attend_slots(
                b, t * FEW, FEW, False, rows_ref, bias_ref, queries_ref, weights, source_ref,
                picked_ref, kv_ref, score_ref, top_ref, total_ref, summed_ref, ones,
            )
            return 0

        lax.fori_loop(0, trips_ref[b], trip, 0)
        return 0

    lax.fori_loop(0, nodes // NODES, block_step, 0)

    mixed_ref[...] = (summed_ref[...] / total_ref[...]).astype(jnp.bfloat16)
    for part in range(2):
        cols = slice(part * half, (part + 1) * half)
        out_rows = pl.ds(3 * width + part * half, half)
        projected = jnp.dot(
            mixed_ref[:, :half], weights_ref[out_rows, :], preferred_element_type=jnp.float32
        ) + jnp.dot(
            mixed_ref[:, half:], peer_weights_ref[out_rows, :], preferred_element_type=jnp.float32
        )
        summed_ref[:, cols] = mesh_ref[:, cols].astype(jnp.float32) + projected
    updated = summed_ref[...]
    mean = jnp.sum(updated, axis=1, keepdims=True) / width
    variance = jnp.sum(updated * updated, axis=1, keepdims=True) / width - mean * mean
    normed = (updated - mean) * lax.rsqrt(variance + EPSILON) * gain_ref[...]
    left = normed[:, :half].astype(jnp.bfloat16)
    right = normed[:, half:].astype(jnp.bfloat16)

    @pl.when(head == 0)
    def _():
        keep_ref[...] = left
        give_ref[...] = right

    @pl.when(head != 0)
    def _():
        keep_ref[...] = right
        give_ref[...] = left


def attend(
    grid_latent,
    mesh_latent,
    neighbours,
    edge_bias,
    query_weight,
    key_weight,
    value_weight,
    out_weight,
    norm_gain,
):
    band, width = grid_latent.shape
    count = mesh_latent.shape[0]
    nodes = count // 2
    half = width // 2
    part = HALO // 2
    head = lax.axis_index("head")
    lat_pos = lax.axis_index("lat")
    lats = lax.axis_size("lat")
    forward = [(i, i + 1) for i in range(lats - 1)]
    backward = [(i + 1, i) for i in range(lats - 1)]
    swap = [(0, 1), (1, 0)]

    low = lax.dynamic_slice_in_dim(grid_latent, band - HALO + head * part, part, 0)
    high = lax.dynamic_slice_in_dim(grid_latent, head * part, part, 0)
    low = lax.ppermute(low, "lat", forward)
    high = lax.ppermute(high, "lat", backward)

    packed = jnp.concatenate(
        [query_weight, key_weight, value_weight, out_weight[:, :half], out_weight[:, half:]],
        axis=0,
    )
    peer_packed = lax.ppermute(packed, "head", swap)
    theirs = lax.dynamic_slice_in_dim(edge_bias, (1 - head) * nodes, nodes, 0)
    mine = lax.dynamic_slice_in_dim(edge_bias, head * nodes, nodes, 0)
    peer_bias = lax.ppermute(theirs, "head", swap)
    peer_gain = lax.ppermute(norm_gain, "head", swap)
    gain = jnp.where(
        head == 0,
        jnp.concatenate([norm_gain, peer_gain]),
        jnp.concatenate([peer_gain, norm_gain]),
    ).astype(jnp.float32)[None, :]

    my_mesh = lax.dynamic_slice_in_dim(mesh_latent, head * nodes, nodes, 0)
    my_neighbours = lax.dynamic_slice_in_dim(neighbours, head * nodes, nodes, 0)
    heads = width // HEAD_DIM
    chunks = width // LANES
    blocks = nodes // NODES
    bias = jnp.concatenate([mine, peer_bias], axis=1).astype(jnp.float32)
    slot_neighbours = my_neighbours.T
    place = slot_neighbours - lat_pos * band
    valid = slot_neighbours >= 0
    inside = valid & (place >= 0) & (place < band)
    outside = valid & ~inside

    def order(rows):
        return (rows * chunks).reshape(K, blocks, NODES).transpose(1, 0, 2).reshape(-1)

    band_rows = order(jnp.where(inside, place, 0))
    band_bias = jnp.where(jnp.tile(inside.T, (1, heads)), bias, -1e30)[None]

    halo_place = jnp.where(place < 0, place + HALO, place - band + HALO)
    slot = jnp.arange(K, dtype=jnp.int32)
    earlier = (slot[:, None] < slot[None, :])[:, :, None]
    rank = jnp.sum(jnp.where(earlier & outside[:, None, :], 1, 0), axis=0)
    found = jnp.sum(outside.astype(jnp.int32), axis=0)
    chosen = outside[:, None, :] & (rank[:, None, :] == slot[None, :, None])
    halo_rows = order(jnp.sum(jnp.where(chosen, halo_place[:, None, :], 0), axis=0))
    slot_bias = bias.T.reshape(heads, K, nodes)
    halo_bias = jnp.sum(jnp.where(chosen[None], slot_bias[:, :, None, :], 0.0), axis=1)
    halo_bias = jnp.where(slot[None, :, None] < found[None, None, :], halo_bias, -1e30)
    halo_bias = halo_bias.reshape(heads, K // FEW, FEW, nodes)
    halo_bias = halo_bias.transpose(1, 3, 0, 2).reshape(K // FEW, nodes, heads * FEW)
    trips = (jnp.max(found.reshape(blocks, NODES), axis=1) + (FEW - 1)) // FEW

    smem = pl.BlockSpec(memory_space=pltpu.SMEM)
    anywhere = pl.BlockSpec(memory_space=pl.ANY)
    vmem = pl.BlockSpec(memory_space=pltpu.VMEM)
    params = pltpu.CompilerParams(vmem_limit_bytes=48 * 1024 * 1024)
    state = jax.ShapeDtypeStruct((nodes, width), jnp.float32)

    def scratch(held, slots):
        return [
            pltpu.VMEM((held * chunks, LANES), jnp.float32),
            pltpu.VMEM((2, STAGE, width), jnp.bfloat16),
            pltpu.VMEM((slots * chunks, LANES), jnp.float32),
            pltpu.VMEM((2, slots, width), jnp.bfloat16),
            pltpu.VMEM((slots, width), jnp.float32),
        ]

    my_mesh, gain, trips, halo_rows, halo_bias = lax.optimization_barrier(
        (my_mesh, gain, trips, halo_rows, halo_bias)
    )
    partial = pl.pallas_call(
        band_kernel,
        out_shape=[state] * 4,
        in_specs=[smem, anywhere] + [vmem] * 4,
        out_specs=[vmem] * 4,
        scratch_shapes=scratch(band, NODES * K) + [pltpu.SemaphoreType.DMA((2,))],
        compiler_params=params,
        name="band",
    )(band_rows, grid_latent, my_mesh, band_bias, packed, peer_packed)

    low_peer = lax.ppermute(low, "head", swap)
    high_peer = lax.ppermute(high, "head", swap)
    out = jax.ShapeDtypeStruct((nodes, half), jnp.bfloat16)
    keep, give = pl.pallas_call(
        halo_kernel,
        out_shape=[out, out],
        in_specs=[smem] * 3 + [anywhere] * 4 + [vmem] * 9,
        out_specs=[vmem, vmem],
        scratch_shapes=scratch(2 * HALO, NODES * FEW)
        + [pltpu.VMEM((nodes, width), jnp.float32)] * 3
        + [pltpu.VMEM((nodes, width), jnp.bfloat16), pltpu.SemaphoreType.DMA((2,))],
        compiler_params=params,
        name="halo",
    )(
        halo_rows, trips, head.reshape(1).astype(jnp.int32), low, low_peer, high, high_peer,
        my_mesh, halo_bias, gain, packed, peer_packed, *partial,
    )
    got = lax.ppermute(give, "head", swap)
    return jnp.where(
        head == 0, jnp.concatenate([keep, got], axis=0), jnp.concatenate([got, keep], axis=0)
    )


def solution(mesh):
    in_specs = (
        P("lat", None),
        P("lat", None),
        P("lat", None),
        P("lat", "head"),
        P(None, "head"),
        P(None, "head"),
        P(None, "head"),
        P("head", None),
        P("head"),
    )
    out_specs = P("lat", "head")
    return jax.shard_map(attend, mesh=mesh, in_specs=in_specs, out_specs=out_specs, check_vma=False)
```

time: 97.3 us -> 122 us (1.25)
  the two profiles are of different devices: /device:TPU:0 before, /device:TPU:17 now
where the time goes in v2:
time: 122 us; the launch traced here: 121 us
  Pallas kernels  54 us (44%)
  waiting for transfers between devices  41.3 us (34%)
  local copies, waits for them, and re-layouts  11.5 us (9%)
  starting transfers between devices  9.68 us (8%)
  other arithmetic  4.17 us (3%)
    pallas_call x1, Pallas kernels, attend(): pl.pallas_call(band_kernel, out_shape=[state] * 4, in_specs=[smem, anywhe...  28.2 us
    pallas_call x1, Pallas kernels, attend(): pl.pallas_call(halo_kernel, out_shape=[out, out], in_specs=[smem] * 3 + [...  25.9 us
    ppermute x1, waiting for transfers between devices, attend(): low = lax.ppermute(low, 'lat', forward)  22.1 us
    ppermute x1, waiting for transfers between devices, attend(): high = lax.ppermute(high, 'lat', backward)  17.8 us
    ppermute x1, starting transfers between devices, attend(): high = lax.ppermute(high, 'lat', backward)  3.95 us
    unnamed x24, local copies, waits for them, and re-layouts  3.2 us
    dynamic_slice x1, local copies, waits for them, and re-layouts, attend(): high = lax.dynamic_slice_in_dim(grid_latent, head * part, part, 0)  3.02 us
  transfers between devices with their start and end apart: 8, of which 3 were waited for; matrix products, arithmetic and copies ran while one was open for 12% of the time, Pallas kernels for 23%

profile of v2, /device:TPU:17, one launch (start us, length us, event | category | flops | bytes accessed | tf_op | source)
XLA Modules:
  0.0 120.9 jit_solution(4664087203380752037)
XLA Ops:
  0.0 0.0 copy-start
  0.0 0.0 copy-start.4
  0.0 0.7 collective-permute-start
  0.7 0.9 constant_dynamic-slice_fusion.2
  1.6 0.1 copy.32
  1.7 0.1 collective-permute-start.1
  1.8 1.0 constant_dynamic-update-slice_fusion.2
  2.8 1.0 constant_dynamic-update-slice_fusion.1
  3.8 1.0 constant_dynamic-update-slice_fusion
  4.8 0.0 copy-done.4
  4.8 0.0 copy-start.1
  4.8 0.5 collective-permute-start.6
  5.3 0.0 copy-start.6
  5.3 0.0 copy-start.8
  5.3 3.0 %constant_dynamic-slice_fusion.3 = (bf16[1024,512]{1,0:T(8,128)(2,1)}, bf16[1024,512]{1,0:T(8,128)(2,1)}) fusion(bf16[8192,512]{1,0:T(8,128)(2,1)} %band_ref.1, s32[]{:T(128)S(6)} %select_n.90, s32[]{:T(128)S(6)} %select_n.89), kind=kLoop, calls=%fused_computation.39 | loop fusion | bytes 4194312 | tf_op jit(solution)/shard_map/dynamic_slice | solution.py:256
  8.4 4.0 %collective-permute-start.4 = (bf16[1024,512]{1,0:T(8,128)(2,1)}, bf16[1024,512]{1,0:T(8,128)(2,1)}, u32[]{:S(2)}, u32[]{:S(2)}) collective-permute-start(bf16[1024,512]{1,0:T(8,128)(2,1)} %get-tuple-element.33), channel_id=1, source_target_pairs={{2,0},{4,2},{6,4},{8,6},{10,8},{12,10},{14,12},{16,14},{18,16},{20... | collective-permute-start | bytes 3145736 | tf_op jit(solution)/shard_map/ppermute | solution.py:258
  12.3 1.9 %collective-permute-start.2 = (bf16[1024,512]{1,0:T(8,128)(2,1)}, bf16[1024,512]{1,0:T(8,128)(2,1)}, u32[]{:S(2)}, u32[]{:S(2)}) collective-permute-start(bf16[1024,512]{1,0:T(8,128)(2,1)} %get-tuple-element.34), channel_id=1, source_target_pairs={{0,2},{2,4},{4,6},{6,8},{8,10},{10,12},{12,14},{14,16},{16,18},{18... | collective-permute-start | bytes 3145736 | tf_op jit(solution)/shard_map/ppermute | solution.py:257
  14.3 0.0 copy-done.6
  14.3 0.1 compare_and_fusion
  14.4 0.1 fusion.2
  14.5 0.1 select_reduce_fusion.2
  14.6 0.0 copy-done.8
  14.7 0.6 concatenate.49
  15.2 0.7 copy.29
  16.0 0.0 copy-start.7
  16.0 0.1 reshape.172
  16.0 0.1 select_reduce_fusion.1
  16.2 0.1 mul.28
  16.2 0.1 reduce_max.9
  16.4 0.0 copy-done
  16.4 0.7 broadcast_compare_fusion
  17.1 0.1 fusion
  17.2 17.8 %collective-permute-done.4.high_ref = bf16[1024,512]{1,0:T(8,128)(2,1)} collective-permute-done((bf16[1024,512]{1,0:T(8,128)(2,1)}, bf16[1024,512]{1,0:T(8,128)(2,1)}, u32[]{:S(2)}, u32[]{:S(2)}) %collective-permute-start.4) | collective-permute-done | bytes 1048608 | tf_op jit(solution)/shard_map/ppermute | solution.py:258
  35.0 1.9 %collective-permute-start.5 = (bf16[1024,512]{1,0:T(8,128)(2,1)}, bf16[1024,512]{1,0:T(8,128)(2,1)}, u32[]{:S(2)}, u32[]{:S(2)}) collective-permute-start(bf16[1024,512]{1,0:T(8,128)(2,1)} %collective-permute-done.4.high_ref), channel_id=1, source_target_pairs={{0,1},{1,0},{2,3},{3,2},{4,5},{5,4},{6,7},{7,6},{8,9},{9,8},{10,11... | collective-permute-start | bytes 3145736 | tf_op jit(solution)/shard_map/ppermute | solution.py:336
  36.9 22.1 %collective-permute-done.2.low_ref = bf16[1024,512]{1,0:T(8,128)(2,1)} collective-permute-done((bf16[1024,512]{1,0:T(8,128)(2,1)}, bf16[1024,512]{1,0:T(8,128)(2,1)}, u32[]{:S(2)}, u32[]{:S(2)}) %collective-permute-start.2) | collective-permute-done | bytes 1048608 | tf_op jit(solution)/shard_map/ppermute | solution.py:257
  59.0 0.5 collective-permute-start.3
  59.5 0.1 reshape.173.rows_ref
  59.6 0.1 reshape.176
  59.7 0.1 reshape.177.rows_ref
  59.7 0.1 copy.31
  59.9 0.0 collective-permute-done
  59.9 0.6 concatenate.50
  60.5 0.0 copy-done.7
  60.5 0.0 collective-permute-done.1
  60.5 0.1 convert_bitcast_fusion
  60.6 0.8 copy.25
  61.4 1.1 select_reduce_fusion
  62.5 0.7 select_bitcast_fusion
  63.3 1.1 copy.30.bias_ref
  64.4 0.0 copy-done.5
  64.4 0.1 convert_select_fusion.bias_ref
  64.5 0.0 copy-start.3
  64.5 0.0 collective-permute-done.6.peer_weights_ref
  64.5 0.0 copy-done.1
  64.5 0.0 copy-start.2
  64.5 28.2 %band.1 = (f32[320,512]{1,0:T(8,128)S(1)}, f32[320,512]{1,0:T(8,128)S(1)}, f32[320,512]{1,0:T(8,128)S(1)}, f32[320,512]{1,0:T(8,128)S(1)}) custom-call(s32[5120]{0:T(1024)S(1)} %reshape.177.rows_ref, bf16[8192,512]{1,0:T(8,128)(2,1)} %band_ref.1, bf16[320,512]{1,0:T(8,128)(2,1)S(1)} %constant_dynamic-slice_fusion.4.mesh_ref, ...), custom_call_target="tpu_custom_call" | custom-call | tf_op jit(solution)/shard_map/band/pallas_call | solution.py:325
  92.7 0.0 copy-done.2
  92.7 0.0 collective-permute-done.5.high_peer_ref
  92.7 0.0 collective-permute-done.3.low_peer_ref
  92.7 0.0 copy-done.3
  92.7 25.9 %halo.1 = (bf16[320,256]{1,0:T(8,128)(2,1)S(1)}, bf16[320,256]{1,0:T(8,128)(2,1)S(1)}) custom-call(s32[5120]{0:T(1024)S(1)} %reshape.173.rows_ref, s32[5]{0:T(128)S(1)} %and_select_fusion.trips_ref, s32[1]{0:T(128)} %bitcast.8.head_ref, bf16[1024,512]{1,0:T(8,128)(2,1)} %collective-permute-done.2.low_ref, ...), custom_call_target="tpu_custom_call" | custom-call | tf_op jit(solution)/shard_map/halo/pallas_call | solution.py:338
  118.6 0.1 collective-permute-start.7
  118.7 1.4 %collective-permute-done.7 = bf16[320,256]{1,0:T(8,128)(2,1)S(1)} collective-permute-done((bf16[320,256]{1,0:T(8,128)(2,1)S(1)}, bf16[320,256]{1,0:T(8,128)(2,1)S(1)}, u32[]{:S(2)}, u32[]{:S(2)}) %collective-permute-start.7) | collective-permute-done | bytes 163872 | tf_op jit(solution)/shard_map/ppermute | solution.py:352
  120.1 0.8 maximum_select_fusion
  (15 shorter events, 0.2 us)
Async XLA Ops:
  0.0 16.4 %copy-start = (bf16[640,512]{1,0:T(8,128)(2,1)S(1)}, bf16[640,512]{1,0:T(8,128)(2,1)}, u32[]{:S(2)}) copy-start(bf16[640,512]{1,0:T(8,128)(2,1)} %param.10) | copy-start | bytes 1966084
  0.0 4.8 %copy-start.4 = (bf16[256,512]{1,0:T(8,128)(2,1)S(1)}, bf16[256,512]{1,0:T(8,128)(2,1)}, u32[]{:S(2)}) copy-start(bf16[256,512]{1,0:T(8,128)(2,1)} %param.16) | copy-start | bytes 786436
  0.0 59.9 %collective-permute-start = (bf16[256]{0:T(256)(128)(2,1)}, bf16[256]{0:T(256)(128)(2,1)}, u32[]{:S(2)}, u32[]{:S(2)}) collective-permute-start(bf16[256]{0:T(256)(128)(2,1)} %param.17), channel_id=1, source_target_pairs={{0,1},{1,0},{2,3},{3,2},{4,5},{5,4},{6,7},{7,6},{8,9},{9,8},{10,11... | collective-permute-start | bytes 1544 | tf_op jit(solution)/shard_map/ppermute | solution.py:268
  1.7 58.8 %collective-permute-start.1 = (bf16[320,32]{1,0:T(8,128)(2,1)S(1)}, bf16[320,32]{1,0:T(8,128)(2,1)S(1)}, u32[]{:S(2)}, u32[]{:S(2)}) collective-permute-start(bf16[320,32]{1,0:T(8,128)(2,1)S(1)} %copy.32), channel_id=1, source_target_pairs={{0,1},{1,0},{2,3},{3,2},{4,5},{5,4},{6,7},{7,6},{8,9},{9,8},{10,11... | collective-permute-start | bytes 61448 | tf_op jit(solution)/shard_map/ppermute | solution.py:267
  4.8 59.7 %copy-start.1 = (bf16[2048,256]{1,0:T(8,128)(2,1)}, bf16[2048,256]{1,0:T(8,128)(2,1)S(1)}, u32[]{:S(2)}) copy-start(bf16[2048,256]{1,0:T(8,128)(2,1)S(1)} %slice_dynamic-update-slice_fusion.weights_ref) | copy-start | bytes 3145732
  4.8 59.7 %collective-permute-start.6 = (bf16[2048,256]{1,0:T(8,128)(2,1)S(1)}, bf16[2048,256]{1,0:T(8,128)(2,1)S(1)}, u32[]{:S(2)}, u32[]{:S(2)}) collective-permute-start(bf16[2048,256]{1,0:T(8,128)(2,1)S(1)} %slice_dynamic-update-slice_fusion.weights_ref), channel_id=1, source_target_pairs={{0,1},{1,0},{2,3},{3,2},{4,5},{5,4},{6,7},{7,6},{8,9},{9,8},{10,11... | collective-permute-start | bytes 3145736 | tf_op jit(solution)/shard_map/ppermute | solution.py:264
  5.3 8.9 %copy-start.6 = (s32[640,16]{0,1:T(8,128)S(1)}, s32[640,16]{0,1:T(8,128)}, u32[]{:S(2)}) copy-start(s32[640,16]{0,1:T(8,128)} %param.11) | copy-start | bytes 122884
  5.3 9.3 %copy-start.8 = (bf16[256]{0:T(256)(128)(2,1)S(1)}, bf16[256]{0:T(256)(128)(2,1)}, u32[]{:S(2)}) copy-start(bf16[256]{0:T(256)(128)(2,1)} %param.17) | copy-start | bytes 1540
  8.4 26.6 %collective-permute-start.4 = (bf16[1024,512]{1,0:T(8,128)(2,1)}, bf16[1024,512]{1,0:T(8,128)(2,1)}, u32[]{:S(2)}, u32[]{:S(2)}) collective-permute-start(bf16[1024,512]{1,0:T(8,128)(2,1)} %get-tuple-element.33), channel_id=1, source_target_pairs={{2,0},{4,2},{6,4},{8,6},{10,8},{12,10},{14,12},{16,14},{18,16},{20... | collective-permute-start | bytes 3145736 | tf_op jit(solution)/shard_map/ppermute | solution.py:258
  12.3 46.7 %collective-permute-start.2 = (bf16[1024,512]{1,0:T(8,128)(2,1)}, bf16[1024,512]{1,0:T(8,128)(2,1)}, u32[]{:S(2)}, u32[]{:S(2)}) collective-permute-start(bf16[1024,512]{1,0:T(8,128)(2,1)} %get-tuple-element.34), channel_id=1, source_target_pairs={{0,2},{2,4},{4,6},{6,8},{8,10},{10,12},{12,14},{14,16},{16,18},{18... | collective-permute-start | bytes 3145736 | tf_op jit(solution)/shard_map/ppermute | solution.py:257
  16.0 44.5 %copy-start.7 = (bf16[1,256]{1,0:T(2,128)(2,1)S(1)}, bf16[1,256]{1,0:T(2,128)(2,1)}, u32[]{:S(2)}) copy-start(bf16[1,256]{1,0:T(2,128)(2,1)} %concatenate.49) | copy-start | bytes 1540
  35.0 57.7 %collective-permute-start.5 = (bf16[1024,512]{1,0:T(8,128)(2,1)}, bf16[1024,512]{1,0:T(8,128)(2,1)}, u32[]{:S(2)}, u32[]{:S(2)}) collective-permute-start(bf16[1024,512]{1,0:T(8,128)(2,1)} %collective-permute-done.4.high_ref), channel_id=1, source_target_pairs={{0,1},{1,0},{2,3},{3,2},{4,5},{5,4},{6,7},{7,6},{8,9},{9,8},{10,11... | collective-permute-start | bytes 3145736 | tf_op jit(solution)/shard_map/ppermute | solution.py:336
  59.0 33.7 %collective-permute-start.3 = (bf16[1024,512]{1,0:T(8,128)(2,1)}, bf16[1024,512]{1,0:T(8,128)(2,1)}, u32[]{:S(2)}, u32[]{:S(2)}) collective-permute-start(bf16[1024,512]{1,0:T(8,128)(2,1)} %collective-permute-done.2.low_ref), channel_id=1, source_target_pairs={{0,1},{1,0},{2,3},{3,2},{4,5},{5,4},{6,7},{7,6},{8,9},{9,8},{10,11... | collective-permute-start | bytes 3145736 | tf_op jit(solution)/shard_map/ppermute | solution.py:335
  61.4 3.0 %copy-start.5 = (pred[1,320,64]{2,1,0:T(8,128)(4,1)S(1)}, pred[1,320,64]{2,1,0:T(8,128)(4,1)}, u32[]{:S(2)}) copy-start(pred[1,320,64]{2,1,0:T(8,128)(4,1)} %copy.29) | copy-start | bytes 61444
  64.5 28.2 %copy-start.3 = (f32[4,320,16]{2,1,0:T(8,128)S(1)}, f32[4,320,16]{2,1,0:T(8,128)}, u32[]{:S(2)}) copy-start(f32[4,320,16]{2,1,0:T(8,128)} %copy.30.bias_ref) | copy-start | bytes 245764
  64.5 28.2 %copy-start.2 = (bf16[2048,256]{1,0:T(8,128)(2,1)}, bf16[2048,256]{1,0:T(8,128)(2,1)S(1)}, u32[]{:S(2)}) copy-start(bf16[2048,256]{1,0:T(8,128)(2,1)S(1)} %collective-permute-done.6.peer_weights_ref) | copy-start | bytes 3145732
  118.6 1.5 %collective-permute-start.7 = (bf16[320,256]{1,0:T(8,128)(2,1)S(1)}, bf16[320,256]{1,0:T(8,128)(2,1)S(1)}, u32[]{:S(2)}, u32[]{:S(2)}) collective-permute-start(bf16[320,256]{1,0:T(8,128)(2,1)S(1)} %get-tuple-element.26), channel_id=1, source_target_pairs={{0,1},{1,0},{2,3},{3,2},{4,5},{5,4},{6,7},{7,6},{8,9},{9,8},{10,11... | collective-permute-start | bytes 491528 | tf_op jit(solution)/shard_map/ppermute | solution.py:352

commit v3 on v2

--- a/solution.py
+++ b/solution.py
@@ -139,8 +139,9 @@
 
 def band_kernel(
     rows_ref, band_ref, mesh_ref, bias_ref, weights_ref, peer_weights_ref,
-    queries_ref, top_ref, total_ref, summed_ref,
-    source_ref, stage_ref, picked_ref, kv_ref, score_ref, sems,
+    queries_out_ref, top_out_ref, total_out_ref, summed_out_ref,
+    source_ref, stage_ref, picked_ref, kv_ref, score_ref,
+    queries_ref, top_ref, total_ref, summed_ref, sems, state_sems,
 ):
     nodes, width = mesh_ref.shape
     half = width // 2
@@ -162,15 +163,30 @@
         return 0
 
     lax.fori_loop(0, nodes // NODES, block_step, 0)
+    copies = [
+        pltpu.make_async_copy(held, out, state_sems.at[n])
+        for n, (held, out) in enumerate(
+            (
+                (queries_ref, queries_out_ref),
+                (top_ref, top_out_ref),
+                (total_ref, total_out_ref),
+                (summed_ref, summed_out_ref),
+            )
+        )
+    ]
+    for copy in copies:
+        copy.start()
+    for copy in copies:
+        copy.wait()
 
 
 def halo_kernel(
     rows_ref, trips_ref, head_ref, low_ref, low_peer_ref, high_ref, high_peer_ref,
-    mesh_ref, bias_ref, gain_ref, weights_ref, peer_weights_ref,
-    queries_ref, top_in_ref, total_in_ref, summed_in_ref,
+    mesh_ref, bias_ref, gain_ref, unsort_ref, weights_ref, peer_weights_ref,
+    queries_in_ref, top_in_ref, total_in_ref, summed_in_ref,
     keep_ref, give_ref,
-    source_ref, stage_ref, picked_ref, kv_ref, score_ref, top_ref, total_ref, summed_ref,
-    mixed_ref, sems,
+    source_ref, stage_ref, picked_ref, kv_ref, score_ref,
+    queries_ref, top_ref, total_ref, summed_ref, sems, state_sems, mixed_ref,
 ):
     nodes, width = mesh_ref.shape
     half = width // 2
@@ -182,10 +198,22 @@
         for p in range(part // STAGE):
             pieces.append((mine, p * STAGE, base + head * part + p * STAGE))
             pieces.append((peer, p * STAGE, base + (1 - head) * part + p * STAGE))
+    copies = [
+        pltpu.make_async_copy(given, held, state_sems.at[n])
+        for n, (given, held) in enumerate(
+            (
+                (queries_in_ref, queries_ref),
+                (top_in_ref, top_ref),
+                (total_in_ref, total_ref),
+                (summed_in_ref, summed_ref),
+            )
+        )
+    ]
+    for copy in copies:
+        copy.start()
     stage(pieces, stage_ref, source_ref, sems)
-    top_ref[...] = top_in_ref[...]
-    total_ref[...] = total_in_ref[...]
-    summed_ref[...] = summed_in_ref[...]
+    for copy in copies:
+        copy.wait()
     ones = head_sums(half)
 
     def block_step(b, _):
@@ -215,8 +243,11 @@
     mean = jnp.sum(updated, axis=1, keepdims=True) / width
     variance = jnp.sum(updated * updated, axis=1, keepdims=True) / width - mean * mean
     normed = (updated - mean) * lax.rsqrt(variance + EPSILON) * gain_ref[...]
-    left = normed[:, :half].astype(jnp.bfloat16)
-    right = normed[:, half:].astype(jnp.bfloat16)
+    normed = jnp.dot(
+        unsort_ref[...], normed.astype(jnp.bfloat16), preferred_element_type=jnp.float32
+    ).astype(jnp.bfloat16)
+    left = normed[:, :half]
+    right = normed[:, half:]
 
     @pl.when(head == 0)
     def _():
@@ -277,8 +308,23 @@
     heads = width // HEAD_DIM
     chunks = width // LANES
     blocks = nodes // NODES
-    bias = jnp.concatenate([mine, peer_bias], axis=1).astype(jnp.float32)
-    slot_neighbours = my_neighbours.T
+    place = my_neighbours - lat_pos * band
+    leaves = (my_neighbours >= 0) & ((place < 0) | (place >= band))
+    number = jnp.arange(nodes, dtype=jnp.int32)
+    weight = jnp.sum(leaves.astype(jnp.int32), axis=1) * nodes + (nodes - 1 - number)
+    before = jnp.sum((weight[:, None] > weight[None, :]).astype(jnp.int32), axis=0)
+    sort = (before[None, :] == number[:, None]).astype(jnp.bfloat16)
+    unsort = (before[:, None] == number[None, :]).astype(jnp.bfloat16)
+    raised = my_neighbours + 1
+    digits = [(raised >> shift) & 255 for shift in (0, 8, 16)]
+    mixed = jnp.concatenate(
+        [my_mesh, mine, peer_bias] + [digit.astype(jnp.bfloat16) for digit in digits], axis=1
+    )
+    mixed = jnp.dot(sort, mixed, preferred_element_type=jnp.float32)
+    my_mesh = mixed[:, :width].astype(jnp.bfloat16)
+    bias = mixed[:, width : width + heads * K]
+    digits = mixed[:, width + heads * K :].astype(jnp.int32).reshape(nodes, 3, K)
+    slot_neighbours = (digits[:, 0] + (digits[:, 1] << 8) + (digits[:, 2] << 16) - 1).T
     place = slot_neighbours - lat_pos * band
     valid = slot_neighbours >= 0
     inside = valid & (place >= 0) & (place < band)
@@ -305,10 +351,12 @@
     trips = (jnp.max(found.reshape(blocks, NODES), axis=1) + (FEW - 1)) // FEW
 
     smem = pl.BlockSpec(memory_space=pltpu.SMEM)
-    anywhere = pl.BlockSpec(memory_space=pl.ANY)
+    anywhere = pl.BlockSpec(memory_space=pltpu.MemorySpace.HBM)
     vmem = pl.BlockSpec(memory_space=pltpu.VMEM)
-    params = pltpu.CompilerParams(vmem_limit_bytes=48 * 1024 * 1024)
-    state = jax.ShapeDtypeStruct((nodes, width), jnp.float32)
+    state = pltpu.HBM((nodes, width), jnp.float32)
+
+    def params(mib):
+        return pltpu.CompilerParams(vmem_limit_bytes=mib * 1024 * 1024)
 
     def scratch(held, slots):
         return [
@@ -317,37 +365,43 @@
             pltpu.VMEM((slots * chunks, LANES), jnp.float32),
             pltpu.VMEM((2, slots, width), jnp.bfloat16),
             pltpu.VMEM((slots, width), jnp.float32),
+        ] + [pltpu.VMEM((nodes, width), jnp.float32)] * 4 + [
+            pltpu.SemaphoreType.DMA((2,)),
+            pltpu.SemaphoreType.DMA((4,)),
         ]
 
-    my_mesh, gain, trips, halo_rows, halo_bias = lax.optimization_barrier(
-        (my_mesh, gain, trips, halo_rows, halo_bias)
-    )
+    my_mesh, gain, trips, halo_rows, halo_bias, unsort = lax.optimization_barrier(
+        (my_mesh, gain, trips, halo_rows, halo_bias, unsort)
+    )
+    held_latent = pltpu.with_memory_space_constraint(grid_latent, pltpu.MemorySpace.HBM)
     partial = pl.pallas_call(
         band_kernel,
         out_shape=[state] * 4,
         in_specs=[smem, anywhere] + [vmem] * 4,
-        out_specs=[vmem] * 4,
-        scratch_shapes=scratch(band, NODES * K) + [pltpu.SemaphoreType.DMA((2,))],
-        compiler_params=params,
+        out_specs=[anywhere] * 4,
+        scratch_shapes=scratch(band, NODES * K),
+        compiler_params=params(40),
         name="band",
-    )(band_rows, grid_latent, my_mesh, band_bias, packed, peer_packed)
+    )(band_rows, held_latent, my_mesh, band_bias, packed, peer_packed)
 
     low_peer = lax.ppermute(low, "head", swap)
     high_peer = lax.ppermute(high, "head", swap)
+    low, low_peer, high, high_peer, *partial = [
+        pltpu.with_memory_space_constraint(array, pltpu.MemorySpace.HBM)
+        for array in (low, low_peer, high, high_peer, *partial)
+    ]
     out = jax.ShapeDtypeStruct((nodes, half), jnp.bfloat16)
     keep, give = pl.pallas_call(
         halo_kernel,
         out_shape=[out, out],
-        in_specs=[smem] * 3 + [anywhere] * 4 + [vmem] * 9,
+        in_specs=[smem] * 3 + [anywhere] * 4 + [vmem] * 6 + [anywhere] * 4,
         out_specs=[vmem, vmem],
-        scratch_shapes=scratch(2 * HALO, NODES * FEW)
-        + [pltpu.VMEM((nodes, width), jnp.float32)] * 3
-        + [pltpu.VMEM((nodes, width), jnp.bfloat16), pltpu.SemaphoreType.DMA((2,))],
-        compiler_params=params,
+        scratch_shapes=scratch(2 * HALO, NODES * FEW) + [pltpu.VMEM((nodes, width), jnp.bfloat16)],
+        compiler_params=params(40),
         name="halo",
     )(
         halo_rows, trips, head.reshape(1).astype(jnp.int32), low, low_peer, high, high_peer,
-        my_mesh, halo_bias, gain, packed, peer_packed, *partial,
+        my_mesh, halo_bias, gain, unsort, packed, peer_packed, *partial,
     )
     got = lax.ppermute(give, "head", swap)
     return jnp.where(

time: 122 us -> 117 us (0.959)
  the two profiles are of different devices: /device:TPU:17 before, /device:TPU:11 now
where the time goes in v3:
time: 117 us; the launch traced here: 116 us
  Pallas kernels  48.5 us (41%)
  waiting for transfers between devices  31.6 us (27%)
  local copies, waits for them, and re-layouts  19.6 us (17%)
  starting transfers between devices  9.48 us (8%)
  other arithmetic  6.15 us (5%)
    pallas_call x1, Pallas kernels, attend(): pl.pallas_call(band_kernel, out_shape=[state] * 4, in_specs=[smem, anywhe...  29.7 us
    ppermute x1, waiting for transfers between devices, attend(): low = lax.ppermute(low, 'lat', forward)  22.4 us
    pallas_call x1, Pallas kernels, attend(): pl.pallas_call(halo_kernel, out_shape=[out, out], in_specs=[smem] * 3 + [...  18.9 us
    ppermute x1, waiting for transfers between devices, attend(): high = lax.ppermute(high, 'lat', backward)  7.77 us
    unnamed x19, local copies, waits for them, and re-layouts  4.96 us
    ppermute x1, starting transfers between devices, attend(): low = lax.ppermute(low, 'lat', forward)  4.02 us
    dynamic_slice x1, local copies, waits for them, and re-layouts, attend(): high = lax.dynamic_slice_in_dim(grid_latent, head * part, part, 0)  3 us
  transfers between devices with their start and end apart: 8, of which 3 were waited for; matrix products, arithmetic and copies ran while one was open for 21% of the time, Pallas kernels for 26%

profile of v3, /device:TPU:11, one launch (start us, length us, event | category | flops | bytes accessed | tf_op | source)
XLA Modules:
  0.0 116.0 jit_solution(7019333453998944682)
XLA Ops:
  0.0 0.0 copy-start
  0.0 0.7 collective-permute-start.1
  0.7 0.9 constant_dynamic-slice_fusion.2
  1.6 0.1 collective-permute-start
  1.7 1.0 constant_dynamic-update-slice_fusion.2
  2.7 1.0 constant_dynamic-update-slice_fusion.1
  3.7 1.0 constant_dynamic-update-slice_fusion
  4.6 0.0 copy-done.3
  4.7 0.5 collective-permute-start.6
  5.2 3.0 %constant_dynamic-slice_fusion = (bf16[1024,512]{1,0:T(8,128)(2,1)}, bf16[1024,512]{1,0:T(8,128)(2,1)}) fusion(bf16[8192,512]{1,0:T(8,128)(2,1)} %band_ref.1, s32[]{:T(128)S(6)} %select_n.83, s32[]{:T(128)S(6)} %select_n.82), kind=kLoop, calls=%fused_computation.56 | loop fusion | bytes 4194312 | tf_op jit(solution)/shard_map/dynamic_slice | solution.py:287
  8.2 2.2 %collective-permute-start.4 = (bf16[1024,512]{1,0:T(8,128)(2,1)}, bf16[1024,512]{1,0:T(8,128)(2,1)}, u32[]{:S(2)}, u32[]{:S(2)}) collective-permute-start(bf16[1024,512]{1,0:T(8,128)(2,1)} %get-tuple-element.33), channel_id=1, source_target_pairs={{2,0},{4,2},{6,4},{8,6},{10,8},{12,10},{14,12},{16,14},{18,16},{20... | collective-permute-start | bytes 3145736 | tf_op jit(solution)/shard_map/ppermute | solution.py:289
  10.4 4.0 %collective-permute-start.2 = (bf16[1024,512]{1,0:T(8,128)(2,1)}, bf16[1024,512]{1,0:T(8,128)(2,1)}, u32[]{:S(2)}, u32[]{:S(2)}) collective-permute-start(bf16[1024,512]{1,0:T(8,128)(2,1)} %get-tuple-element.34), channel_id=1, source_target_pairs={{0,2},{2,4},{4,6},{6,8},{8,10},{10,12},{12,14},{14,16},{16,18},{18... | collective-permute-start | bytes 3145736 | tf_op jit(solution)/shard_map/ppermute | solution.py:288
  14.4 0.0 copy-done.5
  14.4 0.1 convert_reduce_fusion.2
  14.5 0.1 convert_reduce_fusion
  14.7 0.1 fusion.1.unsort_ref
  14.8 0.0 copy-done
  14.8 0.8 constant_dynamic-slice_fusion.4
  15.6 0.0 copy-done.6
  15.6 0.7 copy.45
  16.3 0.1 copy.48
  16.4 0.7 copy.49
  17.2 0.7 copy.47
  17.9 0.0 collective-permute-done.1
  17.9 0.0 collective-permute-done
  17.9 0.7 copy.46
  18.7 1.3 %concatenate.36 = bf16[320,624]{1,0:T(8,128)(2,1)S(1)} concatenate(bf16[320,512]{1,0:T(8,128)(2,1)} %constant_dynamic-slice_fusion.4, bf16[320,32]{1,0:T(8,128)(2,1)} %copy.45, bf16[320,32]{1,0:T(8,128)(2,1)} %copy.46, bf16[320,16]{1,0:T(8,128)(2,1)} %copy.47, bf16[320,16]{1,0:T(8,128)(2,1)S(1)} %copy.48, bf16[320,16]{1,0:T(8,128)(2,1)} %copy.49), dimensions={1} | concatenate | bytes 798720 | tf_op jit(solution)/shard_map/concatenate | solution.py:320
  20.0 0.4 fusion
  20.3 0.0 copy-start.2
  20.3 0.1 slice.34
  20.4 0.8 copy-done.2
  21.3 0.7 copy.58
  22.0 0.9 convert_element_type.42
  22.9 0.7 copy.56
  23.7 0.1 reshape.161
  23.8 0.1 select_reduce_fusion.2
  23.9 0.0 copy-start.4
  23.9 0.1 select_reduce_fusion.1
  24.0 0.5 copy-done.4
  24.5 0.1 mul.46
  24.6 0.1 reshape.162.rows_ref
  24.7 0.1 reshape.165
  24.8 0.1 reshape.166.rows_ref
  24.9 1.6 %select_bitcast_fusion = (f32[1,320,64]{2,1,0:T(8,128)S(1)}, f32[64,320]{0,1:T(8,128)}) fusion(pred[320,64]{1,0:T(8,128)(4,1)} %copy.56, f32[320,624]{1,0:T(8,128)} %copy-done.2), kind=kLoop, calls=%fused_computation.13 | loop fusion | flops 20480 | bytes 266240 | tf_op jit(solution)/shard_map/broadcast_in_dim | solution.py:337
  26.5 1.7 %copy.52 = f32[64,320]{1,0:T(8,128)} copy(f32[64,320]{0,1:T(8,128)} %get-tuple-element.36) | data formatting | bytes 163840 | tf_op jit(solution)/shard_map/transpose | solution.py:346
  28.2 7.8 %collective-permute-done.4.high_ref = bf16[1024,512]{1,0:T(8,128)(2,1)} collective-permute-done((bf16[1024,512]{1,0:T(8,128)(2,1)}, bf16[1024,512]{1,0:T(8,128)(2,1)}, u32[]{:S(2)}, u32[]{:S(2)}) %collective-permute-start.4) | collective-permute-done | bytes 1048608 | tf_op jit(solution)/shard_map/ppermute | solution.py:289
  35.9 1.5 %collective-permute-start.5 = (bf16[1024,512]{1,0:T(8,128)(2,1)}, bf16[1024,512]{1,0:T(8,128)(2,1)}, u32[]{:S(2)}, u32[]{:S(2)}) collective-permute-start(bf16[1024,512]{1,0:T(8,128)(2,1)} %collective-permute-done.4.high_ref), channel_id=1, source_target_pairs={{0,1},{1,0},{2,3},{3,2},{4,5},{5,4},{6,7},{7,6},{8,9},{9,8},{10,11... | collective-permute-start | bytes 3145736 | tf_op jit(solution)/shard_map/ppermute | solution.py:388
  37.4 22.4 %collective-permute-done.2.low_ref = bf16[1024,512]{1,0:T(8,128)(2,1)} collective-permute-done((bf16[1024,512]{1,0:T(8,128)(2,1)}, bf16[1024,512]{1,0:T(8,128)(2,1)}, u32[]{:S(2)}, u32[]{:S(2)}) %collective-permute-start.2) | collective-permute-done | bytes 1048608 | tf_op jit(solution)/shard_map/ppermute | solution.py:288
  59.8 0.4 collective-permute-start.3
  60.3 0.8 fusion.2
  61.1 1.1 select_reduce_fusion
  62.2 0.1 broadcast_compare_fusion.1
  62.3 0.7 copy.54
  63.0 0.1 reduce_max.9
  63.1 2.0 %copy.57.bias_ref = f32[4,320,16]{2,1,0:T(8,128)} copy(f32[4,320,16]{1,0,2:T(4,128)} %bitcast.64) | data formatting | bytes 163840 | tf_op jit(solution)/shard_map/optimization_barrier | solution.py:373
  65.1 0.0 collective-permute-done.6.peer_weights_ref
  65.1 29.7 %band.1 = (f32[320,512]{1,0:T(8,128)}, f32[320,512]{1,0:T(8,128)}, f32[320,512]{1,0:T(8,128)}, f32[320,512]{1,0:T(8,128)}) custom-call(s32[5120]{0:T(1024)S(1)} %reshape.166.rows_ref, bf16[8192,512]{1,0:T(8,128)(2,1)} %band_ref.1, bf16[320,512]{1,0:T(8,128)(2,1)S(1)} %slice.55.mesh_ref, f32[1,320,64]{2,1,0:T(8,128)S(1)} %get-tuple-element.35.bias_ref, ...), custom_call_target="tpu_custom_call" | custom-call | tf_op jit(solution)/shard_map/band/pallas_call | solution.py:377
  94.8 0.0 collective-permute-done.5.high_peer_ref
  94.8 0.0 collective-permute-done.3.low_peer_ref
  94.8 0.0 copy-done.1
  94.8 18.9 %halo.1 = (bf16[320,256]{1,0:T(8,128)(2,1)S(1)}, bf16[320,256]{1,0:T(8,128)(2,1)S(1)}) custom-call(s32[5120]{0:T(1024)S(1)} %reshape.162.rows_ref, s32[5]{0:T(128)S(1)} %and_select_fusion.trips_ref, s32[1]{0:T(128)} %bitcast.13.head_ref, bf16[1024,512]{1,0:T(8,128)(2,1)} %collective-permute-done.2.low_ref, ...), custom_call_target="tpu_custom_call" | custom-call | tf_op jit(solution)/shard_map/halo/pallas_call | solution.py:394
  113.7 0.1 collective-permute-start.7
  113.8 1.4 %collective-permute-done.7 = bf16[320,256]{1,0:T(8,128)(2,1)S(1)} collective-permute-done((bf16[320,256]{1,0:T(8,128)(2,1)S(1)}, bf16[320,256]{1,0:T(8,128)(2,1)S(1)}, u32[]{:S(2)}, u32[]{:S(2)}) %collective-permute-start.7) | collective-permute-done | bytes 163872 | tf_op jit(solution)/shard_map/ppermute | solution.py:406
  115.2 0.9 maximum_select_fusion
  (22 shorter events, 0.3 us)
Async XLA Ops:
  0.0 14.8 %copy-start = (bf16[640,512]{1,0:T(8,128)(2,1)S(1)}, bf16[640,512]{1,0:T(8,128)(2,1)}, u32[]{:S(2)}) copy-start(bf16[640,512]{1,0:T(8,128)(2,1)} %param.10) | copy-start | bytes 1966084
  0.0 4.6 %copy-start.3 = (bf16[256,512]{1,0:T(8,128)(2,1)S(1)}, bf16[256,512]{1,0:T(8,128)(2,1)}, u32[]{:S(2)}) copy-start(bf16[256,512]{1,0:T(8,128)(2,1)} %param.16) | copy-start | bytes 786436
  0.0 17.9 %collective-permute-start.1 = (bf16[256]{0:T(256)(128)(2,1)}, bf16[256]{0:T(256)(128)(2,1)S(1)}, u32[]{:S(2)}, u32[]{:S(2)}) collective-permute-start(bf16[256]{0:T(256)(128)(2,1)} %param.17), channel_id=1, source_target_pairs={{0,1},{1,0},{2,3},{3,2},{4,5},{5,4},{6,7},{7,6},{8,9},{9,8},{10,11... | collective-permute-start | bytes 1544 | tf_op jit(solution)/shard_map/ppermute | solution.py:299
  1.6 16.4 %collective-permute-start = (bf16[320,32]{0,1:T(8,128)(2,1)S(1)}, bf16[320,32]{0,1:T(8,128)(2,1)S(1)}, u32[]{:S(2)}, u32[]{:S(2)}) collective-permute-start(bf16[320,32]{0,1:T(8,128)(2,1)S(1)} %get-tuple-element.41), channel_id=1, source_target_pairs={{0,1},{1,0},{2,3},{3,2},{4,5},{5,4},{6,7},{7,6},{8,9},{9,8},{10,11... | collective-permute-start | bytes 61448 | tf_op jit(solution)/shard_map/ppermute | solution.py:298
  4.7 60.4 %collective-permute-start.6 = (bf16[2048,256]{1,0:T(8,128)(2,1)S(1)}, bf16[2048,256]{1,0:T(8,128)(2,1)S(1)}, u32[]{:S(2)}, u32[]{:S(2)}) collective-permute-start(bf16[2048,256]{1,0:T(8,128)(2,1)S(1)} %slice_dynamic-update-slice_fusion.weights_ref), channel_id=1, source_target_pairs={{0,1},{1,0},{2,3},{3,2},{4,5},{5,4},{6,7},{7,6},{8,9},{9,8},{10,11... | collective-permute-start | bytes 3145736 | tf_op jit(solution)/shard_map/ppermute | solution.py:295
  5.2 9.2 %copy-start.5 = (s32[640,16]{0,1:T(8,128)S(1)}, s32[640,16]{0,1:T(8,128)}, u32[]{:S(2)}) copy-start(s32[640,16]{0,1:T(8,128)} %param.11) | copy-start | bytes 122884
  5.2 10.4 %copy-start.6 = (bf16[256]{0:T(256)(128)(2,1)S(1)}, bf16[256]{0:T(256)(128)(2,1)}, u32[]{:S(2)}) copy-start(bf16[256]{0:T(256)(128)(2,1)} %param.17) | copy-start | bytes 1540
  8.2 27.7 %collective-permute-start.4 = (bf16[1024,512]{1,0:T(8,128)(2,1)}, bf16[1024,512]{1,0:T(8,128)(2,1)}, u32[]{:S(2)}, u32[]{:S(2)}) collective-permute-start(bf16[1024,512]{1,0:T(8,128)(2,1)} %get-tuple-element.33), channel_id=1, source_target_pairs={{2,0},{4,2},{6,4},{8,6},{10,8},{12,10},{14,12},{16,14},{18,16},{20... | collective-permute-start | bytes 3145736 | tf_op jit(solution)/shard_map/ppermute | solution.py:289
  10.4 49.5 %collective-permute-start.2 = (bf16[1024,512]{1,0:T(8,128)(2,1)}, bf16[1024,512]{1,0:T(8,128)(2,1)}, u32[]{:S(2)}, u32[]{:S(2)}) collective-permute-start(bf16[1024,512]{1,0:T(8,128)(2,1)} %get-tuple-element.34), channel_id=1, source_target_pairs={{0,2},{2,4},{4,6},{6,8},{8,10},{10,12},{12,14},{14,16},{16,18},{18... | collective-permute-start | bytes 3145736 | tf_op jit(solution)/shard_map/ppermute | solution.py:288
  20.3 0.9 copy-start.2
  23.9 0.6 copy-start.4
  35.9 58.9 %collective-permute-start.5 = (bf16[1024,512]{1,0:T(8,128)(2,1)}, bf16[1024,512]{1,0:T(8,128)(2,1)}, u32[]{:S(2)}, u32[]{:S(2)}) collective-permute-start(bf16[1024,512]{1,0:T(8,128)(2,1)} %collective-permute-done.4.high_ref), channel_id=1, source_target_pairs={{0,1},{1,0},{2,3},{3,2},{4,5},{5,4},{6,7},{7,6},{8,9},{9,8},{10,11... | collective-permute-start | bytes 3145736 | tf_op jit(solution)/shard_map/ppermute | solution.py:388
  59.8 35.0 %collective-permute-start.3 = (bf16[1024,512]{1,0:T(8,128)(2,1)}, bf16[1024,512]{1,0:T(8,128)(2,1)}, u32[]{:S(2)}, u32[]{:S(2)}) collective-permute-start(bf16[1024,512]{1,0:T(8,128)(2,1)} %collective-permute-done.2.low_ref), channel_id=1, source_target_pairs={{0,1},{1,0},{2,3},{3,2},{4,5},{5,4},{6,7},{7,6},{8,9},{9,8},{10,11... | collective-permute-start | bytes 3145736 | tf_op jit(solution)/shard_map/ppermute | solution.py:387
  65.1 29.7 %copy-start.1 = (f32[4,320,16]{2,1,0:T(8,128)S(1)}, f32[4,320,16]{2,1,0:T(8,128)}, u32[]{:S(2)}) copy-start(f32[4,320,16]{2,1,0:T(8,128)} %copy.57.bias_ref) | copy-start | bytes 245764
  113.7 1.5 %collective-permute-start.7 = (bf16[320,256]{1,0:T(8,128)(2,1)S(1)}, bf16[320,256]{1,0:T(8,128)(2,1)S(1)}, u32[]{:S(2)}, u32[]{:S(2)}) collective-permute-start(bf16[320,256]{1,0:T(8,128)(2,1)S(1)} %get-tuple-element.28), channel_id=1, source_target_pairs={{0,1},{1,0},{2,3},{3,2},{4,5},{5,4},{6,7},{7,6},{8,9},{9,8},{10,11... | collective-permute-start | bytes 491528 | tf_op jit(solution)/shard_map/ppermute | solution.py:406
